TPU v7x, 32 devices: a whole 2x2x4 slice. The times are simulated.
32 devices in a mesh: spin: 2 (over x), band: 16 (over z, y, core).
Axes of the slice: x: 2, y: 2, z: 4, core: 2. Of those that a mesh axis runs over, the one named last changes fastest.
Arguments:
- orbitals: bfloat16 [32, 262144], P(('spin', 'band')), parts along dimension 0, may hold values from -6 to 6
- trial: bfloat16 [32, 262144], P(('spin', 'band')), parts along dimension 0, may hold values from -6 to 6
- occupations: int32 [32], P(('spin', 'band')), parts along dimension 0, may hold values 0 or 1
Outputs:
- exchange: bfloat16 [32, 262144], P(('spin', 'band')), parts along dimension 0
- projected: bfloat16 [32, 262144], P('spin', 'band'), parts along dimension 0
There are 2 independent parts, one for each index of `spin`. A program takes and returns all parts, laid end to end along the dimension named above; each array names one. Nothing has to cross between parts.
All inputs are finite; a program needn't handle non-finite values. No bound on the sum of `occupations` on one device may be relied on, other than what follows from the above.
Results may differ from a plain program's by a relative error of at most 0.018.
Values may be sent and summed in bfloat16 or wider, within the bound.
A program may use at most 64 MiB of HBM per device.

v0:
```python
import functools
import math

import jax
import jax.numpy as jnp
from jax import lax
from jax.experimental import pallas as pl
from jax.experimental.pallas import tpu as pltpu
from jax.sharding import PartitionSpec as P

NG = 64
FRACTION = 0.25
OMEGA = 1.0
CHUNK = 2048
MESH = pl.DeviceIdType.MESH


def passed_along(value, axis, steps):
    count = lax.axis_size(axis)
    pairs = [(source, (source + steps) % count) for source in range(count)]
    return lax.ppermute(value, axis, pairs)


def cas_table(extent):
    indices = jnp.arange(extent, dtype=jnp.int32)
    products = indices[:, None] * indices[None, :] % extent
    phases = products.astype(jnp.float32) * (2.0 * math.pi / extent)
    return (jnp.cos(phases) + jnp.sin(phases)).astype(jnp.bfloat16)


def screened_kernel(extent):
    modes = jnp.arange(extent, dtype=jnp.int32)
    modes = jnp.where(2 * modes < extent, modes, modes - extent)
    wavenum = modes.astype(jnp.float32) * (2.0 * math.pi / extent)
    squares = wavenum * wavenum
    norm_sq = squares[:, None, None] + squares[None, :, None] + squares[None, None, :]
    bounded = jnp.where(norm_sq > 0, norm_sq, 1.0)
    screened = jnp.where(
        norm_sq > 0,
        4.0 * math.pi / bounded * (1.0 - jnp.exp(-bounded / (4.0 * OMEGA * OMEGA))),
        math.pi / (OMEGA * OMEGA),
    )
    return screened / extent**3


def screened_potential(values, table, kernel):
    patterns = ("ga,abc->gbc", "gb,abc->agc", "gc,abc->abg")
    for pattern in patterns:
        values = jnp.einsum(pattern, table, values, preferred_element_type=jnp.float32).astype(
            jnp.bfloat16
        )
    values = (values.astype(jnp.float32) * kernel).astype(jnp.bfloat16)
    for ordinal, pattern in enumerate(patterns):
        values = jnp.einsum(pattern, table, values, preferred_element_type=jnp.float32)
        if ordinal < 2:
            values = values.astype(jnp.bfloat16)
    return values


def greet(count, me):
    barrier = pltpu.get_barrier_semaphore()

    @pl.loop(1, count)
    def _(step):
        peer = lax.rem(me + step, count)
        pl.semaphore_signal(barrier, inc=1, device_id={"band": peer}, device_id_type=MESH)

    pl.semaphore_wait(barrier, count - 1)


def slabs_body(count, arrays, *refs):
    ins, outs = refs[:arrays], refs[arrays : 2 * arrays]
    send_sem, recv_sem, own_sem = refs[2 * arrays :]
    me = lax.axis_index("band")
    greet(count, me)

    def remote(which, peer, slot):
        return pltpu.make_async_remote_copy(
            src_ref=ins[which].at[peer],
            dst_ref=outs[which].at[slot],
            send_sem=send_sem.at[which, peer],
            recv_sem=recv_sem.at[which, slot],
            device_id={"band": peer},
            device_id_type=MESH,
        )

    def own(which):
        return pltpu.make_async_copy(ins[which].at[me], outs[which].at[me], own_sem.at[which])

    for which in range(arrays):

        @pl.loop(1, count)
        def _(step):
            remote(which, lax.rem(me + step, count), me).start()

        own(which).start()
    for which in range(arrays):
        own(which).wait()

        @pl.loop(1, count)
        def _(step):
            remote(which, lax.rem(me + step, count), me).wait_send()

        @pl.loop(1, count)
        def _(step):
            peer = lax.rem(me + count - step, count)
            remote(which, peer, peer).wait_recv()


def to_slabs(arrays, collective_id):
    count = lax.axis_size("band")
    number = len(arrays)
    shape = arrays[0].shape
    size = math.prod(shape)
    return pl.pallas_call(
        functools.partial(slabs_body, count, number),
        out_shape=[jax.ShapeDtypeStruct(shape, a.dtype) for a in arrays],
        in_specs=[pl.BlockSpec(memory_space=pltpu.VMEM)] * number,
        out_specs=[pl.BlockSpec(memory_space=pltpu.VMEM)] * number,
        scratch_shapes=[
            pltpu.SemaphoreType.DMA((number, count)),
            pltpu.SemaphoreType.DMA((number, count)),
            pltpu.SemaphoreType.DMA((number,)),
        ],
        cost_estimate=pl.CostEstimate(
            flops=0, bytes_accessed=size * 40 * number, transcendentals=0
        ),
        compiler_params=pltpu.CompilerParams(
            collective_id=collective_id, has_side_effects=True
        ),
        name="to_slabs",
    )(*arrays)


def summed_body(count, part_ref, total_ref, parts, send_sem, recv_sem):
    me = lax.axis_index("band")
    greet(count, me)

    def remote(peer, slot):
        return pltpu.make_async_remote_copy(
            src_ref=part_ref,
            dst_ref=parts.at[slot],
            send_sem=send_sem.at[peer],
            recv_sem=recv_sem.at[slot],
            device_id={"band": peer},
            device_id_type=MESH,
        )

    @pl.loop(1, count)
    def _(step):
        remote(lax.rem(me + step, count), me).start()

    parts[pl.ds(me, 1)] = part_ref[...][None]

    @pl.loop(1, count)
    def _(step):
        remote(lax.rem(me + step, count), me).wait_send()

    @pl.loop(1, count)
    def _(step):
        peer = lax.rem(me + count - step, count)
        remote(peer, peer).wait_recv()

    total_ref[...] = jnp.sum(parts[...], axis=0)


def summed(part, collective_id):
    count = lax.axis_size("band")
    return pl.pallas_call(
        functools.partial(summed_body, count),
        out_shape=jax.ShapeDtypeStruct(part.shape, part.dtype),
        in_specs=[pl.BlockSpec(memory_space=pltpu.VMEM)],
        out_specs=pl.BlockSpec(memory_space=pltpu.VMEM),
        scratch_shapes=[
            pltpu.VMEM((count,) + part.shape, part.dtype),
            pltpu.SemaphoreType.DMA((count,)),
            pltpu.SemaphoreType.DMA((count,)),
        ],
        compiler_params=pltpu.CompilerParams(
            collective_id=collective_id, has_side_effects=True
        ),
        name="summed",
    )(part)


def rows_body(chunk, *refs):
    half = len(refs) // 2
    for line, rows in zip(refs[:half], refs[half:]):

        @pl.loop(0, line.shape[1] // chunk, unroll=4)
        def _(step):
            cut = pl.ds(pl.multiple_of(step * chunk, chunk), chunk)
            out = pl.ds(pl.multiple_of(step * (chunk // 128), chunk // 128), chunk // 128)
            wide = line[:, cut].astype(jnp.float32).reshape(chunk // 128, 128)
            rows[out, :] = wide.astype(rows.dtype)


def as_rows(*lines):
    number = len(lines)
    cells = lines[0].shape[1]
    return pl.pallas_call(
        functools.partial(rows_body, CHUNK),
        out_shape=[jax.ShapeDtypeStruct((cells // 128, 128), a.dtype) for a in lines],
        in_specs=[pl.BlockSpec(memory_space=pltpu.VMEM)] * number,
        out_specs=[pl.BlockSpec(memory_space=pltpu.VMEM)] * number,
        cost_estimate=pl.CostEstimate(
            flops=0, bytes_accessed=cells * 16 * number, transcendentals=0
        ),
        name="as_rows",
    )(*lines)


def local(orbitals, trial, occupations):
    count = lax.axis_size("band")
    cells = orbitals.shape[1]
    extent = NG
    table = cas_table(extent)
    kernel = screened_kernel(extent)
    cube = (extent, extent, extent)
    fill = occupations.astype(jnp.bfloat16)

    (lined,) = as_rows(orbitals)
    (trial_rows,) = as_rows(trial)
    visitor, visitor_fill = passed_along((lined, fill), "band", 1)
    own = lined.reshape(cube).astype(jnp.float32)
    own_weighted = own * fill[0].astype(jnp.float32)
    own_potential = screened_potential((own * own).astype(jnp.bfloat16), table, kernel)
    accumulated = own_potential * own_weighted

    other = visitor.reshape(cube).astype(jnp.float32)
    potential = screened_potential((own * other).astype(jnp.bfloat16), table, kernel)
    carried = passed_along((potential * own_weighted).astype(jnp.bfloat16), "band", -1)
    accumulated = accumulated + potential * (other * visitor_fill[0].astype(jnp.float32))
    accumulated = accumulated + carried.astype(jnp.float32)
    exchange = (-FRACTION * accumulated).astype(jnp.bfloat16).reshape(1, cells)

    slab = (count, cells // count // 128, 128)
    grid_exchange, grid_trial = to_slabs((exchange.reshape(slab), trial_rows.reshape(slab)), 1)
    grid_exchange = grid_exchange.reshape(count, -1)
    grid_trial = grid_trial.reshape(count, -1)
    part = lax.dot_general(
        grid_exchange, grid_trial, (((1,), (1,)), ((), ())), preferred_element_type=jnp.float32
    )
    intersection_low = (summed(part, 2) / math.sqrt(cells)).astype(jnp.bfloat16)
    projected = -(
        lax.dot_general(
            intersection_low,
            grid_exchange,
            (((0,), (0,)), ((), ())),
            preferred_element_type=jnp.float32,
        )
        / math.sqrt(count)
    )
    return (exchange, projected.astype(jnp.bfloat16))


def solution(mesh):
    return jax.shard_map(
        local,
        mesh=mesh,
        in_specs=(P(("spin", "band"), None), P(("spin", "band"), None), P(("spin", "band"))),
        out_specs=(P(("spin", "band"), None), P("spin", "band")),
        check_vma=False,
    )
```

profile of v0, /device:TPU:0, one launch (start us, length us, event | category | flops | bytes accessed | tf_op | source)
XLA Modules:
  0.0 96.8 jit_solution(2446618162544193886)
XLA Ops:
  0.6 2.4 %as_rows.2 = bf16[2048,128]{1,0:T(8,128)(2,1)} custom-call(bf16[1,262144]{1,0:T(2,128)(2,1)} %refs_0_.2), custom_call_target="tpu_custom_call" | custom-call | bytes 4194304 | tf_op jit(solution)/shard_map/as_rows/pallas_call | solution.py:201
  3.1 0.5 collective-permute-start
  4.2 3.6 %collective-permute-start.1 = (bf16[1]{0:T(256)(128)(2,1)}, bf16[1]{0:T(256)(128)(2,1)}, u32[]{:S(2)}, u32[]{:S(2)}) collective-permute-start(bf16[1]{0:T(256)(128)(2,1)} %convert_element_type.186), channel_id=1, source_target_pairs={{0,1},{1,2},{2,3},{3,4},{4,5},{5,6},{6,7},{7,8},{8,9},{9,10},{10,1... | collective-permute-start | bytes 14 | tf_op jit(solution)/shard_map/ppermute | solution.py:21
  7.8 2.4 %as_rows.3 = bf16[2048,128]{1,0:T(8,128)(2,1)} custom-call(bf16[1,262144]{1,0:T(2,128)(2,1)} %refs_0_.3), custom_call_target="tpu_custom_call" | custom-call | bytes 4194304 | tf_op jit(solution)/shard_map/as_rows/pallas_call | solution.py:201
  10.3 0.1 broadcast_add_fusion
  10.3 5.4 %collective-permute-done.1 = bf16[1]{0:T(256)(128)(2,1)} collective-permute-done((bf16[1]{0:T(256)(128)(2,1)}, bf16[1]{0:T(256)(128)(2,1)}, u32[]{:S(2)}, u32[]{:S(2)}) %collective-permute-start.1) | collective-permute-done | bytes 34 | tf_op jit(solution)/shard_map/ppermute | solution.py:21
  16.3 0.0 collective-permute-done
  16.3 2.5 %fusion.16 = (bf16[2048,128]{1,0:T(8,128)(2,1)}, f32[2048,128]{1,0:T(8,128)}, bf16[2048,128]{1,0:T(8,128)(2,1)S(1)}, f32[2048,128]{1,0:T(8,128)S(1)}) fusion(bf16[2048,128]{1,0:T(8,128)(2,1)} %as_rows.2, f32[]{:T(128)S(6)} %convert.2, bf16[2048,128]{1,0:T(8,128)(2,1)S(1)} %collective-permute-done, f32[]{:T(128)S(6)} %convert.3), kind=kLoop, calls=%fused_computation.38 | loop fusion | flops 2097152 | bytes 4194312 | tf_op jit(solution)/shard_map/convert_element_type | solution.py:227
  18.8 0.4 convert_element_type.191
  19.2 1.0 %fusion.20 = bf16[64,64,64]{2,0,1:T(8,128)(2,1)S(1)} fusion(bf16[64,64,64]{2,1,0:T(8,128)(2,1)S(1)} %convert_element_type.191), kind=kOutput, calls=%fused_computation.42 | convolution fusion | flops 33619968 | bytes 1048576 | tf_op jit(solution)/shard_map/ga,abc->gbc/dot_general | solution.py:49
  20.2 2.2 %multiply_convert_fusion.2 = bf16[64,64,64]{2,1,0:T(8,128)(2,1)S(1)} fusion(bf16[64,64,64]{2,0,1:T(8,128)(2,1)S(1)} %fusion.20, f32[64]{0:T(128)S(1)} %fusion.88, f32[64,64]{1,0:T(8,128)S(1)} %broadcast_add_fusion), kind=kOutput, calls=%fused_computation.19 | convolution fusion | flops 71172096 | bytes 1065216 | tf_op jit(solution)/shard_map/gc,abc->abg/dot_general | solution.py:49
  22.3 2.0 %fusion.18 = bf16[64,64,64]{2,0,1:T(8,128)(2,1)} fusion(bf16[64,64,64]{2,1,0:T(8,128)(2,1)S(1)} %multiply_convert_fusion.2), kind=kOutput, calls=%fused_computation.40 | convolution fusion | flops 33619968 | bytes 1048576 | tf_op jit(solution)/shard_map/ga,abc->gbc/dot_general | solution.py:54
  24.4 1.6 %mul.231 = f32[64,64,64]{2,1,0:T(8,128)S(1)} reshape(f32[2048,128]{1,0:T(8,128)} %get-tuple-element.7) | data formatting | bytes 2097152 | tf_op jit(solution)/shard_map/mul | solution.py:226
  25.9 4.2 %multiply_convert_fusion.1 = (bf16[64,64,64]{2,1,0:T(8,128)(2,1)}, f32[64,64,64]{2,1,0:T(8,128)}) fusion(f32[64,64,64]{2,1,0:T(8,128)S(1)} %mul.231, bf16[64,64,64]{2,0,1:T(8,128)(2,1)} %fusion.18), kind=kOutput, calls=%fused_computation.18 | convolution fusion | flops 68026368 | bytes 3145728 | tf_op jit(solution)/shard_map/gc,abc->abg/dot_general | solution.py:54
  30.1 1.8 %collective-permute-start.2 = (bf16[64,64,64]{2,1,0:T(8,128)(2,1)}, bf16[64,64,64]{2,1,0:T(8,128)(2,1)}, u32[]{:S(2)}, u32[]{:S(2)}) collective-permute-start(bf16[64,64,64]{2,1,0:T(8,128)(2,1)} %get-tuple-element.10), channel_id=1, source_target_pairs={{0,15},{1,0},{2,1},{3,2},{4,3},{5,4},{6,5},{7,6},{8,7},{9,8},{10,9... | collective-permute-start | bytes 1572872 | tf_op jit(solution)/shard_map/ppermute | solution.py:21
  31.9 2.4 %convert_element_type.175 = bf16[64,64,64]{2,1,0:T(8,128)(2,1)} reshape(bf16[2048,128]{1,0:T(8,128)(2,1)} %get-tuple-element.6) | data formatting | bytes 1048576 | tf_op jit(solution)/shard_map/convert_element_type | solution.py:227
  34.2 3.2 %fusion.24 = bf16[64,64,64]{2,0,1:T(8,128)(2,1)} fusion(bf16[64,64,64]{2,1,0:T(8,128)(2,1)} %convert_element_type.175), kind=kOutput, calls=%fused_computation.46 | convolution fusion | flops 33619968 | bytes 1048576 | tf_op jit(solution)/shard_map/ga,abc->gbc/dot_general | solution.py:49
  37.5 4.3 %multiply_convert_fusion.3 = bf16[64,64,64]{2,1,0:T(8,128)(2,1)} fusion(bf16[64,64,64]{2,0,1:T(8,128)(2,1)} %fusion.24, f32[64]{0:T(128)S(1)} %fusion.88, f32[64,64]{1,0:T(8,128)S(1)} %broadcast_add_fusion), kind=kOutput, calls=%fused_computation.20 | convolution fusion | flops 71172096 | bytes 1065216 | tf_op jit(solution)/shard_map/gc,abc->abg/dot_general | solution.py:49
  41.8 1.6 %mul.237 = f32[64,64,64]{2,1,0:T(8,128)} reshape(f32[2048,128]{1,0:T(8,128)S(1)} %get-tuple-element.9) | data formatting | bytes 2097152 | tf_op jit(solution)/shard_map/mul | solution.py:233
  43.5 2.2 %fusion.22 = bf16[64,64,64]{2,0,1:T(8,128)(2,1)S(1)} fusion(bf16[64,64,64]{2,1,0:T(8,128)(2,1)} %multiply_convert_fusion.3), kind=kOutput, calls=%fused_computation.44 | convolution fusion | flops 33619968 | bytes 1048576 | tf_op jit(solution)/shard_map/ga,abc->gbc/dot_general | solution.py:54
  45.7 2.6 %fusion.13 = f32[64,64,64]{2,1,0:T(8,128)} fusion(bf16[64,64,64]{2,0,1:T(8,128)(2,1)S(1)} %fusion.22), kind=kOutput, calls=%fused_computation.33 | convolution fusion | flops 67502080 | bytes 1572864 | tf_op jit(solution)/shard_map/gc,abc->abg/dot_general | solution.py:54
  48.3 0.0 collective-permute-done.2
  48.3 4.3 %multiply_convert_fusion = bf16[64,64,64]{2,1,0:T(8,128)(2,1)S(1)} fusion(bf16[64,64,64]{2,1,0:T(8,128)(2,1)} %collective-permute-done.2, f32[64,64,64]{2,1,0:T(8,128)} %get-tuple-element.11, f32[64,64,64]{2,1,0:T(8,128)} %mul.237, f32[64,64,64]{2,1,0:T(8,128)} %fusion.13, f32[64,64,64]{2,1,0:T(8,128)S(1)} %mul.231), kind=kLoop, calls=%fused_computation.17 | loop fusion | flops 1835008 | bytes 5242880 | tf_op jit(solution)/shard_map/convert_element_type | solution.py:235
  52.6 1.3 %reshape_reshape.3.refs_0_ = bf16[16,128,128]{2,1,0:T(8,128)(2,1)} reshape(bf16[64,64,64]{2,1,0:T(8,128)(2,1)S(1)} %multiply_convert_fusion) | data formatting | bytes 1048576 | tf_op jit(solution)/shard_map/reshape;reshape | solution.py:238
  53.9 1.5 %reshape.98 = bf16[1,262144]{1,0:T(2,128)(2,1)} reshape(bf16[64,64,64]{2,1,0:T(8,128)(2,1)S(1)} %multiply_convert_fusion) | data formatting | bytes 1048576 | tf_op jit(solution)/shard_map/reshape | solution.py:235
  55.4 25.7 %to_slabs.1 = (bf16[16,128,128]{2,1,0:T(8,128)(2,1)}, bf16[16,128,128]{2,1,0:T(8,128)(2,1)}) custom-call(bf16[16,128,128]{2,1,0:T(8,128)(2,1)} %reshape_reshape.3.refs_0_, bf16[16,128,128]{2,1,0:T(8,128)(2,1)} %bitcast.51), custom_call_target="tpu_custom_call" | custom-call | bytes 20971520 | tf_op jit(solution)/shard_map/to_slabs/pallas_call | solution.py:115
  81.1 2.5 %convolution_bitcast_fusion.part_ref = f32[16,16]{1,0:T(8,128)} fusion(bf16[16,128,128]{2,1,0:T(8,128)(2,1)} %get-tuple-element.5, bf16[16,128,128]{2,1,0:T(8,128)(2,1)} %get-tuple-element.4), kind=kOutput, calls=%fused_computation.37 | convolution fusion | flops 8388608 | bytes 1049600 | tf_op jit(solution)/shard_map/dot_general | solution.py:241
  83.6 10.8 %summed.1 = f32[16,16]{1,0:T(8,128)} custom-call(f32[16,16]{1,0:T(8,128)} %convolution_bitcast_fusion.part_ref), custom_call_target="tpu_custom_call" | custom-call | tf_op jit(solution)/shard_map/summed/pallas_call | solution.py:169
  94.5 2.3 %fusion.1 = bf16[16,16384]{1,0:T(8,128)(2,1)} fusion(bf16[2,8,128,128]{3,2,1,0:T(8,128)(2,1)} %bitcast.52, f32[16,16]{1,0:T(8,128)} %summed.1), kind=kOutput, calls=%fused_computation.2 | convolution fusion | flops 9175552 | bytes 1049600 | tf_op jit(solution)/shard_map/dot_general | solution.py:246
  (1 shorter events, 0.0 us)
Async XLA Ops:
  3.1 13.2 %collective-permute-start = (bf16[2048,128]{1,0:T(8,128)(2,1)}, bf16[2048,128]{1,0:T(8,128)(2,1)S(1)}, u32[]{:S(2)}, u32[]{:S(2)}) collective-permute-start(bf16[2048,128]{1,0:T(8,128)(2,1)} %as_rows.2), channel_id=1, source_target_pairs={{0,1},{1,2},{2,3},{3,4},{4,5},{5,6},{6,7},{7,8},{8,9},{9,10},{10,1... | collective-permute-start | bytes 1572872 | tf_op jit(solution)/shard_map/ppermute | solution.py:21
  4.2 11.5 %collective-permute-start.1 = (bf16[1]{0:T(256)(128)(2,1)}, bf16[1]{0:T(256)(128)(2,1)}, u32[]{:S(2)}, u32[]{:S(2)}) collective-permute-start(bf16[1]{0:T(256)(128)(2,1)} %convert_element_type.186), channel_id=1, source_target_pairs={{0,1},{1,2},{2,3},{3,4},{4,5},{5,6},{6,7},{7,8},{8,9},{9,10},{10,1... | collective-permute-start | bytes 14 | tf_op jit(solution)/shard_map/ppermute | solution.py:21
  30.1 18.2 %collective-permute-start.2 = (bf16[64,64,64]{2,1,0:T(8,128)(2,1)}, bf16[64,64,64]{2,1,0:T(8,128)(2,1)}, u32[]{:S(2)}, u32[]{:S(2)}) collective-permute-start(bf16[64,64,64]{2,1,0:T(8,128)(2,1)} %get-tuple-element.10), channel_id=1, source_target_pairs={{0,15},{1,0},{2,1},{3,2},{4,3},{5,4},{6,5},{7,6},{8,7},{9,8},{10,9... | collective-permute-start | bytes 1572872 | tf_op jit(solution)/shard_map/ppermute | solution.py:21
where the time goes:
time: 97.3 us; the launch traced here: 96.8 us
  Pallas kernels  41.4 us (43%)
  matrix products  26.6 us (27%)
  local copies, waits for them, and re-layouts  8.77 us (9%)
  other arithmetic  6.8 us (7%)
  starting transfers between devices  5.87 us (6%)
  waiting for transfers between devices  5.39 us (6%)
  between operations  1.91 us (2%)
    pallas_call x1, Pallas kernels, to_slabs(): pl.pallas_call(functools.partial(slabs_body, count, number), out_shape=[j...  25.7 us
    dot_general x8, matrix products, screened_potential(): jnp.einsum(pattern, table, values, preferred_element_type=jnp.float32)  21.8 us
    pallas_call x1, Pallas kernels, summed(): pl.pallas_call(functools.partial(summed_body, count), out_shape=jax.Shape...  10.8 us
    ppermute x3, starting transfers between devices, passed_along(): return lax.ppermute(value, axis, pairs)  5.87 us
    ppermute x3, waiting for transfers between devices, passed_along(): return lax.ppermute(value, axis, pairs)  5.39 us
    pallas_call x2, Pallas kernels, as_rows(): pl.pallas_call(functools.partial(rows_body, CHUNK), out_shape=[jax.ShapeD...  4.85 us
    convert_element_type x1, other arithmetic, local(): exchange = (-FRACTION * accumulated).astype(jnp.bfloat16).reshape(1, cells)  4.26 us
    dot_general x1, matrix products, local(): lax.dot_general(grid_exchange, grid_trial, (((1,), (1,)), ((), ())), pref...  2.51 us
  transfers between devices with their start and end apart: 3, of which 1 were waited for; matrix products, arithmetic and copies ran while one was open for 17% of the time, Pallas kernels for 2%

commit v1 on v0

v1 whole, which is shorter than its diff:
```python
import functools
import math

import jax
import jax.numpy as jnp
import numpy as np
from jax import lax
from jax.experimental import pallas as pl
from jax.experimental.pallas import tpu as pltpu
from jax.sharding import PartitionSpec as P

NG = 64
FRACTION = 0.25
OMEGA = 1.0
LANES = 128
TILE = 256
CHUNKS = 4
MESH = pl.DeviceIdType.MESH

HALF = NG // 2
PLANE = NG * NG
ROWS = NG * NG * NG // LANES


def cas_table():
    index = np.arange(NG)
    phases = (index[:, None] * index[None, :] % NG).astype(np.float32) * np.float32(2.0 * math.pi / NG)
    return np.cos(phases) + np.sin(phases)


def tables():
    table = cas_table()
    order = np.concatenate([np.arange(0, NG, 2), np.arange(1, NG, 2)])
    eye = np.eye(TILE // NG, dtype=np.float32)
    left_a = np.kron(eye, table)
    left_b = np.kron(eye, table[order][:, order])
    right_c = np.kron(np.eye(LANES // NG, dtype=np.float32), table)
    return [jnp.asarray(t).astype(jnp.bfloat16) for t in (left_a, left_b, right_c)]


def dot(left, right):
    return jnp.dot(left, right, preferred_element_type=jnp.float32)


def low(value):
    return value.astype(jnp.bfloat16)


def wide(value):
    return value.astype(jnp.float32)


def exchanged(first, second):
    lower = lax.broadcasted_iota(jnp.int32, first.shape, 1) < LANES // 2
    return (
        jnp.where(lower, first, pltpu.roll(second, LANES // 2, 1)),
        jnp.where(lower, pltpu.roll(first, LANES // 2, 1), second),
    )


def wavenum_sq(index):
    modes = wide(jnp.where(2 * index < NG, index, index - NG))
    wavenum = modes * (2.0 * math.pi / NG)
    return wavenum * wavenum


def screened_rows(group):
    shape = (TILE, LANES)
    row = lax.broadcasted_iota(jnp.int32, shape, 0)
    lane = lax.broadcasted_iota(jnp.int32, shape, 1)
    a = row % NG
    b = 2 * (group * (TILE // NG) + row // NG) + lane // NG
    norm_sq = wavenum_sq(a) + wavenum_sq(b) + wavenum_sq(lane % NG)
    bounded = jnp.where(norm_sq > 0, norm_sq, 1.0)
    screened = jnp.where(
        norm_sq > 0,
        4.0 * math.pi / bounded * (1.0 - jnp.exp(-bounded / (4.0 * OMEGA * OMEGA))),
        math.pi / (OMEGA * OMEGA),
    )
    return screened * (1.0 / NG**3)


def partner(me, step, count):
    total, bit = 0, 1
    while bit < count:
        total = total + bit * ((me // bit + step // bit) % 2)
        bit *= 2
    return total


def body(
    count,
    orb_hbm, tri_hbm, occ, left_a, left_b, right_c,
    exch_hbm, proj_hbm,
    orb_line, tri_line, own, own_w, sibling, remote, tri_rows, kern, field, acc,
    e_rows, t_in, e_in, tt, et, part, parts, exch_line, proj,
    load_sem, orb_send, orb_recv, t_send, t_recv, e_send, e_recv, p_send, p_recv, out_sem,
):
    me = lax.axis_index("band")
    barrier = pltpu.get_barrier_semaphore()
    slab = ROWS // count
    pack = TILE // count
    spread = LANES // count
    groups = slab // pack
    tiles = ROWS // TILE
    per_tile = TILE // NG

    load_orb = pltpu.make_async_copy(orb_hbm, orb_line, load_sem.at[0])
    load_tri = pltpu.make_async_copy(tri_hbm, tri_line, load_sem.at[1])
    load_orb.start()
    load_tri.start()

    @pl.loop(1, count)
    def _(step):
        pl.semaphore_signal(
            barrier, inc=1, device_id={"band": partner(me, step, count)}, device_id_type=MESH
        )

    def plane(ref, a):
        cut = pl.ds(pl.multiple_of(a * PLANE, PLANE), PLANE)
        return wide(ref[:, cut]).reshape(PLANE // LANES, LANES)

    fill = occ[0].astype(jnp.float32)
    load_orb.wait()

    @pl.loop(0, HALF)
    def _(a):
        pair = jnp.concatenate(exchanged(plane(orb_line, a), plane(orb_line, a + HALF)), axis=0)
        cut = pl.ds(pl.multiple_of(a * NG, NG), NG)
        own[cut, :] = low(pair)
        own_w[cut, :] = low(pair * fill)

    load_tri.wait()
    flat_rows = tri_rows.reshape(ROWS, LANES)

    @pl.loop(0, NG)
    def _(a):
        flat_rows[pl.ds(pl.multiple_of(a * (PLANE // LANES), PLANE // LANES), PLANE // LANES), :] = low(
            plane(tri_line, a)
        )

    sib = me + 1 - 2 * (me % 2)
    rem = (me + count - 1 + 2 * (me % 2)) % count
    depth = ROWS // CHUNKS

    def orbital(side, chunk):
        cut = pl.ds(chunk * depth, depth)
        return pltpu.make_async_remote_copy(
            src_ref=own_w.at[cut],
            dst_ref=(sibling, remote)[side].at[cut],
            send_sem=orb_send.at[side, chunk],
            recv_sem=orb_recv.at[side, chunk],
            device_id={"band": (sib, rem)[side]},
            device_id_type=MESH,
        )

    def slab_copy(src, dst, send, recv, peer, slot):
        return pltpu.make_async_remote_copy(
            src_ref=src,
            dst_ref=dst.at[slot],
            send_sem=send.at[peer],
            recv_sem=recv.at[slot],
            device_id={"band": peer},
            device_id_type=MESH,
        )

    def trial_copy(peer, slot):
        return slab_copy(tri_rows.at[peer], t_in, t_send, t_recv, peer, slot)

    def exchange_copy(peer, slot):
        return slab_copy(e_rows.at[peer], e_in, e_send, e_recv, peer, slot)

    def part_copy(peer, slot):
        return slab_copy(part, parts, p_send, p_recv, peer, slot)

    pl.semaphore_wait(barrier, count - 1)
    for chunk in range(CHUNKS):
        orbital(1, chunk).start()
    for chunk in range(CHUNKS):
        orbital(0, chunk).start()

    def send_trial(low_bits):
        @pl.loop(0, count // 4)
        def _(i):
            for bits in low_bits:
                step = (count // 4 - 1 - i) * 4 + bits
                peer = partner(me, step, count)
                if bits == 0:

                    @pl.when(i < count // 4 - 1)
                    def _():
                        trial_copy(peer, me).start()
                else:
                    trial_copy(peer, me).start()

    send_trial((0, 1))

    @pl.loop(0, tiles)
    def _(group):
        kern[pl.ds(pl.multiple_of(group * TILE, TILE), TILE), :] = screened_rows(group)

    def tile(group):
        return pl.ds(pl.multiple_of(group * TILE, TILE), TILE)

    def rise(weighted, start, stop):
        @pl.loop(start, stop)
        def _(group):
            cut = tile(group)
            density = low(wide(own[cut, :]) * wide(weighted[cut, :]))
            field[cut, :] = dot(left_b[...], low(dot(density, right_c[...])))

    def turn():
        @pl.loop(0, tiles)
        def _(group):
            pieces = []
            for j in range(per_tile):
                b = group * per_tile + j
                pieces += exchanged(
                    field[pl.ds(b, HALF, stride=NG), :], field[pl.ds(b + HALF, HALF, stride=NG), :]
                )
            value = low(dot(left_a[...], low(jnp.concatenate(pieces, axis=0))))
            value = low(wide(value) * kern[tile(group), :])
            value = low(dot(left_a[...], value))
            value = dot(value, right_c[...])
            for j in range(per_tile):
                b = group * per_tile + j
                first, second = exchanged(
                    value[j * NG : j * NG + HALF], value[j * NG + HALF : (j + 1) * NG]
                )
                field[pl.ds(b, HALF, stride=NG), :] = first
                field[pl.ds(b + HALF, HALF, stride=NG), :] = second

    def fall(weighted, group):
        cut = tile(group)
        return dot(left_b[...], low(field[cut, :])) * wide(weighted[cut, :])

    rise(own_w, 0, tiles)
    turn()

    @pl.loop(0, tiles)
    def _(group):
        acc[tile(group), :] = fall(own_w, group)

    for chunk in range(CHUNKS):
        orbital(0, chunk).wait_recv()
    rise(sibling, 0, tiles)
    turn()

    @pl.loop(0, tiles)
    def _(group):
        acc[tile(group), :] += fall(sibling, group)

    for chunk in range(CHUNKS):
        orbital(1, chunk).wait_recv()
        rise(remote, chunk * tiles // CHUNKS, (chunk + 1) * tiles // CHUNKS)
    send_trial((2, 3))
    turn()
    flat_e = e_rows.reshape(ROWS, LANES)

    @pl.loop(0, tiles)
    def _(group):
        value = -FRACTION * (acc[tile(group), :] + fall(remote, group))
        for j in range(per_tile):
            a = group * per_tile + j
            first, second = exchanged(
                value[j * NG : j * NG + HALF], value[j * NG + HALF : (j + 1) * NG]
            )
            flat_e[pl.ds(pl.multiple_of(a * HALF, HALF), HALF), :] = low(first)
            flat_e[pl.ds(pl.multiple_of((a + HALF) * HALF, HALF), HALF), :] = low(second)

    t_in[pl.ds(me, 1)] = tri_rows[pl.ds(me, 1)]
    e_in[pl.ds(me, 1)] = e_rows[pl.ds(me, 1)]

    @pl.loop(1, count)
    def _(i):
        peer = partner(me, count - i, count)
        exchange_copy(peer, me).start()

    @pl.loop(0, NG)
    def _(a):
        cut = pl.ds(pl.multiple_of(a * PLANE, PLANE), PLANE)
        rows = wide(flat_e[pl.ds(pl.multiple_of(a * HALF, HALF), HALF), :])
        exch_line[:, cut] = low(rows.reshape(1, PLANE))

    store_exch = pltpu.make_async_copy(exch_line, exch_hbm, out_sem.at[0])
    store_exch.start()

    def spread_out(src, dst, slot):
        dst[pl.ds(slot, slab, stride=count), :] = wide(src[slot])

    spread_out(t_in, tt, me)

    @pl.loop(1, count)
    def _(i):
        peer = partner(me, count - i, count)
        trial_copy(peer, peer).wait_recv()
        spread_out(t_in, tt, peer)

    spread_out(e_in, et, me)

    @pl.loop(1, count)
    def _(i):
        peer = partner(me, i, count)
        exchange_copy(peer, peer).wait_recv()
        spread_out(e_in, et, peer)

    def side_by_side(ref):
        return jnp.concatenate([low(ref[g * TILE : (g + 1) * TILE, :]) for g in range(groups)], axis=1)

    gram = lax.dot_general(
        side_by_side(tt), side_by_side(et), (((1,), (1,)), ((), ())), preferred_element_type=jnp.float32
    )
    column = lax.broadcasted_iota(jnp.int32, (count, TILE), 1) // count
    total = jnp.zeros((count, TILE), jnp.float32)
    for r in range(pack):
        total = total + jnp.where(column == r, gram[r * count : (r + 1) * count], 0.0)
    total = total[:, :LANES] + total[:, LANES:]
    shift = LANES // 2
    while shift >= count:
        total = total + pltpu.roll(total, shift, 1)
        shift //= 2
    here = (
        lax.broadcasted_iota(jnp.int32, (count, LANES), 0) % spread
        == lax.broadcasted_iota(jnp.int32, (count, LANES), 1) // count
    )
    if spread > 1:
        total = jnp.sum(
            jnp.where(here, total, 0.0).reshape(count // spread, spread, LANES), axis=1
        )
    part[...] = total
    parts[pl.ds(me, 1)] = total[None]

    @pl.loop(1, count)
    def _(i):
        part_copy(partner(me, count - i, count), me).start()

    @pl.loop(1, count)
    def _(i):
        peer = partner(me, i, count)
        part_copy(peer, peer).wait_recv()

    total = jnp.sum(parts[...], axis=0) / math.sqrt(ROWS * LANES)
    if spread > 1:
        total = jnp.broadcast_to(total[:, None, :], (count // spread, spread, LANES)).reshape(
            count, LANES
        )
        total = jnp.where(here, total, 0.0)
        shift = LANES // 2
        while shift >= count:
            total = total + pltpu.roll(total, shift, 1)
            shift //= 2
    total = jnp.concatenate([total, total], axis=1)
    mixing = low(
        jnp.concatenate([jnp.where(column == r, total, 0.0) for r in range(pack)], axis=0)
    )
    for group in range(groups):
        piece = dot(mixing, low(et[group * TILE : (group + 1) * TILE, :]))
        piece = low(piece * (-1.0 / math.sqrt(count)))
        for r in range(pack):
            at = (group * pack + r) * LANES
            proj[:, at : at + LANES] = piece[r * count : (r + 1) * count]
    store_proj = pltpu.make_async_copy(proj, proj_hbm, out_sem.at[1])
    store_proj.start()

    for chunk in range(CHUNKS):
        for side in range(2):
            orbital(side, chunk).wait_send()

    @pl.loop(1, count)
    def _(i):
        peer = partner(me, i, count)
        trial_copy(peer, me).wait_send()
        exchange_copy(peer, me).wait_send()
        part_copy(peer, me).wait_send()

    store_exch.wait()
    store_proj.wait()


def local(orbitals, trial, occupations):
    count = lax.axis_size("band")
    cells = orbitals.shape[1]
    slab = ROWS // count
    rows = (ROWS, LANES)
    bf16, f32 = jnp.bfloat16, jnp.float32
    spread = LANES // count
    compact = (count // spread, LANES)
    dma = pltpu.SemaphoreType.DMA
    anywhere = pl.BlockSpec(memory_space=pl.ANY)
    vmem = pl.BlockSpec(memory_space=pltpu.VMEM)
    return pl.pallas_call(
        functools.partial(body, count),
        out_shape=(
            jax.ShapeDtypeStruct((1, cells), bf16),
            jax.ShapeDtypeStruct((count, cells // count), bf16),
        ),
        in_specs=[anywhere, anywhere, pl.BlockSpec(memory_space=pltpu.SMEM), vmem, vmem, vmem],
        out_specs=(anywhere, anywhere),
        scratch_shapes=[
            pltpu.VMEM((1, cells), bf16),
            pltpu.VMEM((1, cells), bf16),
            pltpu.VMEM(rows, bf16),
            pltpu.VMEM(rows, bf16),
            pltpu.VMEM(rows, bf16),
            pltpu.VMEM(rows, bf16),
            pltpu.VMEM((count, slab, LANES), bf16),
            pltpu.VMEM(rows, f32),
            pltpu.VMEM(rows, f32),
            pltpu.VMEM(rows, f32),
            pltpu.VMEM((count, slab, LANES), bf16),
            pltpu.VMEM((count, slab, LANES), bf16),
            pltpu.VMEM((count, slab, LANES), bf16),
            pltpu.VMEM(rows, f32),
            pltpu.VMEM(rows, f32),
            pltpu.VMEM(compact, f32),
            pltpu.VMEM((count,) + compact, f32),
            pltpu.VMEM((1, cells), bf16),
            pltpu.VMEM((count, cells // count), bf16),
            dma((2,)),
            dma((2, CHUNKS)),
            dma((2, CHUNKS)),
            dma((count,)),
            dma((count,)),
            dma((count,)),
            dma((count,)),
            dma((count,)),
            dma((count,)),
            dma((2,)),
        ],
        compiler_params=pltpu.CompilerParams(collective_id=1, has_side_effects=True),
        name="exchange_and_projection",
    )(orbitals, trial, occupations, *tables())


def solution(mesh):
    return jax.shard_map(
        local,
        mesh=mesh,
        in_specs=(P(("spin", "band"), None), P(("spin", "band"), None), P(("spin", "band"))),
        out_specs=(P(("spin", "band"), None), P("spin", "band")),
        check_vma=False,
    )
```

time: 97.3 us -> 67.2 us (0.69)
  matrix products: 26.6 us -> 0 us
  Pallas kernels: 41.4 us -> 61.9 us
  other arithmetic: 6.8 us -> 0 us
  starting transfers between devices: 5.87 us -> 0 us
  waiting for transfers between devices: 5.39 us -> 0 us
  local copies, waits for them, and re-layouts: 8.77 us -> 3.79 us
    dot_general x10 -> x0, matrix products: 26.6 us -> none  [the longest x8 21.8 us: screened_potential(): jnp.einsum(pattern, table, values, preferred_element_type=jnp.float32)]
    pallas_call x4 -> x1, Pallas kernels: 41.4 us -> 61.9 us  [local(): pl.pallas_call(functools.partial(body, count), out_shape=(jax.ShapeDtypeS...]
    convert_element_type x2 -> x0, other arithmetic: 6.72 us -> none  [the longest x1 4.26 us: local(): exchange = (-FRACTION * accumulated).astype(jnp.bfloat16).reshape(1, cells)]
    ppermute x3 -> x0, starting transfers between devices: 5.87 us -> none  [passed_along(): return lax.ppermute(value, axis, pairs)]
    ppermute x3 -> x0, waiting for transfers between devices: 5.39 us -> none  [passed_along(): return lax.ppermute(value, axis, pairs)]
    unnamed x0 -> x4, local copies, waits for them, and re-layouts: none -> 3.79 us
    mul x2 -> x0, local copies, waits for them, and re-layouts: 3.22 us -> none  [the longest x1 1.64 us: local(): other * visitor_fill[0].astype(jnp.float32)]
    convert_element_type x2 -> x0, local copies, waits for them, and re-layouts: 2.76 us -> none  [the longest x1 2.36 us: local(): (own * own).astype(jnp.bfloat16)]
  transfers between devices with their start and end apart: 3 -> 0, of which waited for: 1 -> 0; matrix products, arithmetic and copies ran while one was open for 17% -> 0% of each run, Pallas kernels for 2% -> 0%
where the time goes in v1:
time: 67.2 us; the launch traced here: 67 us
  Pallas kernels  61.9 us (92%)
  local copies, waits for them, and re-layouts  3.79 us (6%)
  between operations  1.29 us (2%)
    pallas_call x1, Pallas kernels, local(): pl.pallas_call(functools.partial(body, count), out_shape=(jax.ShapeDtypeS...  61.9 us
    unnamed x4, local copies, waits for them, and re-layouts  3.79 us

profile of v1, /device:TPU:0, one launch (start us, length us, event | category | flops | bytes accessed | tf_op | source)
XLA Modules:
  0.0 67.0 jit_solution(11491431357332517876)
XLA Ops:
  1.3 61.9 %exchange_and_projection.1 = (bf16[1,262144]{1,0:T(2,128)(2,1)}, bf16[16,16384]{1,0:T(8,128)(2,1)}) custom-call(bf16[1,262144]{1,0:T(2,128)(2,1)} %orb_hbm.1, bf16[1,262144]{1,0:T(2,128)(2,1)} %tri_hbm.1, s32[1]{0:T(128)S(6)} %copy.10.occ, bf16[256,256]{1,0:T(8,128)(2,1)} %constant.12.left_a, bf16[256,256]{1,0:T(8,128)(2,1)} %constant.13.left_b, ...), custom_call_target="tpu_custom_call" | custom-call | tf_op jit(solution)/shard_map/exchange_and_projection/pallas_call | solution.py:391
  63.2 0.0 copy-start
  63.2 3.0 %copy.11 = bf16[1,262144]{1,0:T(2,128)(2,1)} copy(bf16[1,262144]{1,0:T(2,128)(2,1)} %get-tuple-element.4) | data formatting | bytes 1048576
  66.2 0.0 copy-done
  66.2 0.8 %copy.12 = bf16[16,16384]{1,0:T(8,128)(2,1)} copy(bf16[16,16384]{1,0:T(8,128)(2,1)S(1)} %copy-done) | data formatting | bytes 1048576
Async XLA Ops:
  63.2 3.0 %copy-start = (bf16[16,16384]{1,0:T(8,128)(2,1)S(1)}, bf16[16,16384]{1,0:T(8,128)(2,1)}, u32[]{:S(2)}) copy-start(bf16[16,16384]{1,0:T(8,128)(2,1)} %get-tuple-element.5) | copy-start | bytes 1572868

commit v2 on v1

--- a/solution.py
+++ b/solution.py
@@ -15,9 +15,11 @@
 LANES = 128
 TILE = 256
 CHUNKS = 4
+UNROLL = 2
 MESH = pl.DeviceIdType.MESH
 
 HALF = NG // 2
+SUB = TILE // HALF
 PLANE = NG * NG
 ROWS = NG * NG * NG // LANES
 
@@ -32,10 +34,14 @@
     table = cas_table()
     order = np.concatenate([np.arange(0, NG, 2), np.arange(1, NG, 2)])
     eye = np.eye(TILE // NG, dtype=np.float32)
-    left_a = np.kron(eye, table)
+    sums = np.array([[1.0, 1.0], [1.0, -1.0]], np.float32)
+    right_c = np.kron(np.eye(TILE // LANES, dtype=np.float32), np.kron(sums, table))
     left_b = np.kron(eye, table[order][:, order])
-    right_c = np.kron(np.eye(LANES // NG, dtype=np.float32), table)
-    return [jnp.asarray(t).astype(jnp.bfloat16) for t in (left_a, left_b, right_c)]
+    halves = (table[0::2, :HALF], table[1::2, :HALF])
+    rows = np.eye(TILE // HALF, dtype=np.float32)
+    left_a = np.concatenate([np.kron(half, rows) for half in halves])
+    back_a = np.concatenate([np.kron(half.T, rows) for half in halves])
+    return [jnp.asarray(t).astype(jnp.bfloat16) for t in (left_a, back_a, left_b, right_c)]
 
 
 def dot(left, right):
@@ -68,8 +74,9 @@
     shape = (TILE, LANES)
     row = lax.broadcasted_iota(jnp.int32, shape, 0)
     lane = lax.broadcasted_iota(jnp.int32, shape, 1)
-    a = row % NG
-    b = 2 * (group * (TILE // NG) + row // NG) + lane // NG
+    a = 2 * (row // SUB) + lane // NG
+    place = group * SUB + row % SUB
+    b = 2 * (place % HALF) + place // HALF
     norm_sq = wavenum_sq(a) + wavenum_sq(b) + wavenum_sq(lane % NG)
     bounded = jnp.where(norm_sq > 0, norm_sq, 1.0)
     screened = jnp.where(
@@ -90,7 +97,7 @@
 
 def body(
     count,
-    orb_hbm, tri_hbm, occ, left_a, left_b, right_c,
+    orb_hbm, tri_hbm, occ, left_a, back_a, left_b, right_c,
     exch_hbm, proj_hbm,
     orb_line, tri_line, own, own_w, sibling, remote, tri_rows, kern, field, acc,
     e_rows, t_in, e_in, tt, et, part, parts, exch_line, proj,
@@ -130,8 +137,8 @@
         own[cut, :] = low(pair)
         own_w[cut, :] = low(pair * fill)
 
+    flat_rows = tri_rows.reshape(ROWS, LANES)
     load_tri.wait()
-    flat_rows = tri_rows.reshape(ROWS, LANES)
 
     @pl.loop(0, NG)
     def _(a):
@@ -202,53 +209,69 @@
     def tile(group):
         return pl.ds(pl.multiple_of(group * TILE, TILE), TILE)
 
+    def two(read, step):
+        return jnp.concatenate([read(2 * step), read(2 * step + 1)], axis=1)
+
+    def halved(value):
+        lane = lax.broadcasted_iota(jnp.int32, (TILE, TILE), 1)
+        return jnp.where(lane % LANES < LANES // 2, value[:TILE], value[TILE:])
+
     def rise(weighted, start, stop):
-        @pl.loop(start, stop)
-        def _(group):
-            cut = tile(group)
-            density = low(wide(own[cut, :]) * wide(weighted[cut, :]))
-            field[cut, :] = dot(left_b[...], low(dot(density, right_c[...])))
+        @pl.loop(start // 2, stop // 2, unroll=min(UNROLL, (stop - start) // 2))
+        def _(step):
+            density = two(
+                lambda group: low(wide(own[tile(group), :]) * wide(weighted[tile(group), :])), step
+            )
+            value = dot(left_b[...], low(dot(density, right_c[...])))
+            field[tile(2 * step), :] = value[:, :LANES]
+            field[tile(2 * step + 1), :] = value[:, LANES:]
+
+    def strip(a, group):
+        return pl.ds(pl.multiple_of(a * NG + group * SUB, SUB), SUB)
 
     def turn():
-        @pl.loop(0, tiles)
-        def _(group):
-            pieces = []
-            for j in range(per_tile):
-                b = group * per_tile + j
-                pieces += exchanged(
-                    field[pl.ds(b, HALF, stride=NG), :], field[pl.ds(b + HALF, HALF, stride=NG), :]
-                )
-            value = low(dot(left_a[...], low(jnp.concatenate(pieces, axis=0))))
-            value = low(wide(value) * kern[tile(group), :])
-            value = low(dot(left_a[...], value))
+        @pl.loop(0, tiles // 2, unroll=UNROLL)
+        def _(step):
+            value = two(
+                lambda group: low(
+                    jnp.concatenate([field[strip(a, group), :] for a in range(HALF)], axis=0)
+                ),
+                step,
+            )
+            value = low(halved(dot(left_a[...], value)))
+            value = low(wide(value) * two(lambda group: kern[tile(group), :], step))
+            value = low(halved(dot(back_a[...], value)))
             value = dot(value, right_c[...])
-            for j in range(per_tile):
-                b = group * per_tile + j
-                first, second = exchanged(
-                    value[j * NG : j * NG + HALF], value[j * NG + HALF : (j + 1) * NG]
-                )
-                field[pl.ds(b, HALF, stride=NG), :] = first
-                field[pl.ds(b + HALF, HALF, stride=NG), :] = second
-
-    def fall(weighted, group):
-        cut = tile(group)
-        return dot(left_b[...], low(field[cut, :])) * wide(weighted[cut, :])
+            for side in range(2):
+                for a in range(HALF):
+                    field[strip(a, 2 * step + side), :] = value[
+                        a * SUB : (a + 1) * SUB, side * LANES : (side + 1) * LANES
+                    ]
+
+    def fall(weighted, step):
+        value = dot(left_b[...], two(lambda group: low(field[tile(group), :]), step))
+        return [
+            value[:, side * LANES : (side + 1) * LANES] * wide(weighted[tile(2 * step + side), :])
+            for side in range(2)
+        ]
 
     rise(own_w, 0, tiles)
     turn()
 
-    @pl.loop(0, tiles)
-    def _(group):
-        acc[tile(group), :] = fall(own_w, group)
+    @pl.loop(0, tiles // 2, unroll=UNROLL)
+    def _(step):
+        for side, value in enumerate(fall(own_w, step)):
+            acc[tile(2 * step + side), :] = value
 
     for chunk in range(CHUNKS):
         orbital(0, chunk).wait_recv()
     rise(sibling, 0, tiles)
     turn()
 
-    @pl.loop(0, tiles)
-    def _(group):
-        acc[tile(group), :] += fall(sibling, group)
+    @pl.loop(0, tiles // 2, unroll=UNROLL)
+    def _(step):
+        for side, value in enumerate(fall(sibling, step)):
+            acc[tile(2 * step + side), :] += value
 
     for chunk in range(CHUNKS):
         orbital(1, chunk).wait_recv()
@@ -257,16 +280,18 @@
     turn()
     flat_e = e_rows.reshape(ROWS, LANES)
 
-    @pl.loop(0, tiles)
-    def _(group):
-        value = -FRACTION * (acc[tile(group), :] + fall(remote, group))
-        for j in range(per_tile):
-            a = group * per_tile + j
-            first, second = exchanged(
-                value[j * NG : j * NG + HALF], value[j * NG + HALF : (j + 1) * NG]
-            )
-            flat_e[pl.ds(pl.multiple_of(a * HALF, HALF), HALF), :] = low(first)
-            flat_e[pl.ds(pl.multiple_of((a + HALF) * HALF, HALF), HALF), :] = low(second)
+    @pl.loop(0, tiles // 2, unroll=UNROLL)
+    def _(step):
+        for side, value in enumerate(fall(remote, step)):
+            group = 2 * step + side
+            value = -FRACTION * (acc[tile(group), :] + value)
+            for j in range(per_tile):
+                a = group * per_tile + j
+                first, second = exchanged(
+                    value[j * NG : j * NG + HALF], value[j * NG + HALF : (j + 1) * NG]
+                )
+                flat_e[pl.ds(pl.multiple_of(a * HALF, HALF), HALF), :] = low(first)
+                flat_e[pl.ds(pl.multiple_of((a + HALF) * HALF, HALF), HALF), :] = low(second)
 
     t_in[pl.ds(me, 1)] = tri_rows[pl.ds(me, 1)]
     e_in[pl.ds(me, 1)] = e_rows[pl.ds(me, 1)]
@@ -394,7 +419,7 @@
             jax.ShapeDtypeStruct((1, cells), bf16),
             jax.ShapeDtypeStruct((count, cells // count), bf16),
         ),
-        in_specs=[anywhere, anywhere, pl.BlockSpec(memory_space=pltpu.SMEM), vmem, vmem, vmem],
+        in_specs=[anywhere, anywhere, pl.BlockSpec(memory_space=pltpu.SMEM), vmem, vmem, vmem, vmem],
         out_specs=(anywhere, anywhere),
         scratch_shapes=[
             pltpu.VMEM((1, cells), bf16),

time: 67.2 us -> 51.2 us (0.76)
  Pallas kernels: 61.9 us -> 46 us
    pallas_call x1, Pallas kernels: 61.9 us -> 46 us  [local(): pl.pallas_call(functools.partial(body, count), out_shape=(jax.ShapeDtypeS...]
where the time goes in v2:
time: 51.2 us; the launch traced here: 51 us
  Pallas kernels  46 us (90%)
  local copies, waits for them, and re-layouts  3.79 us (7%)
  between operations  1.29 us (3%)
    pallas_call x1, Pallas kernels, local(): pl.pallas_call(functools.partial(body, count), out_shape=(jax.ShapeDtypeS...  46 us
    unnamed x4, local copies, waits for them, and re-layouts  3.79 us

profile of v2, /device:TPU:0, one launch (start us, length us, event | category | flops | bytes accessed | tf_op | source)
XLA Modules:
  0.0 51.0 jit_solution(6341050324899612447)
XLA Ops:
  1.3 46.0 %exchange_and_projection.1 = (bf16[1,262144]{1,0:T(2,128)(2,1)}, bf16[16,16384]{1,0:T(8,128)(2,1)}) custom-call(bf16[1,262144]{1,0:T(2,128)(2,1)} %orb_hbm.1, bf16[1,262144]{1,0:T(2,128)(2,1)} %tri_hbm.1, s32[1]{0:T(128)S(6)} %copy.11.occ, bf16[512,256]{1,0:T(8,128)(2,1)} %constant.15.left_a, bf16[512,256]{1,0:T(8,128)(2,1)} %constant.16.back_a, ...), custom_call_target="tpu_custom_call" | custom-call | tf_op jit(solution)/shard_map/exchange_and_projection/pallas_call | solution.py:416
  47.2 0.0 copy-start
  47.2 3.0 %copy.12 = bf16[1,262144]{1,0:T(2,128)(2,1)} copy(bf16[1,262144]{1,0:T(2,128)(2,1)} %get-tuple-element.4) | data formatting | bytes 1048576
  50.2 0.0 copy-done
  50.2 0.8 %copy.13 = bf16[16,16384]{1,0:T(8,128)(2,1)} copy(bf16[16,16384]{1,0:T(8,128)(2,1)S(1)} %copy-done) | data formatting | bytes 1048576
Async XLA Ops:
  47.2 3.0 %copy-start = (bf16[16,16384]{1,0:T(8,128)(2,1)S(1)}, bf16[16,16384]{1,0:T(8,128)(2,1)}, u32[]{:S(2)}) copy-start(bf16[16,16384]{1,0:T(8,128)(2,1)} %get-tuple-element.5) | copy-start | bytes 1572868

commit v3 on v2

v3 whole, which is shorter than its diff:
```python
import functools
import math

import jax
import jax.numpy as jnp
import numpy as np
from jax import lax
from jax.experimental import pallas as pl
from jax.experimental.pallas import tpu as pltpu
from jax.sharding import PartitionSpec as P

NG = 64
FRACTION = 0.25
OMEGA = 1.0
LANES = 128
TILE = 256
CHUNKS = 4
UNROLL = 2
LAST_UNROLL = 2
VMEM_LIMIT = 30 << 20
WRITTEN_OUT = 32
ORBITAL, SIBLING, TRIAL, RELAY, ONWARD, EXCHANGE, PART = range(7)
KINDS = 7
MESH = pl.DeviceIdType.MESH

HALF = NG // 2
SUB = TILE // HALF
PLANE = NG * NG
ROWS = NG * NG * NG // LANES


def cas_table():
    index = np.arange(NG)
    phases = (index[:, None] * index[None, :] % NG).astype(np.float32) * np.float32(2.0 * math.pi / NG)
    return np.cos(phases) + np.sin(phases)


def tables():
    table = cas_table()
    order = np.concatenate([np.arange(0, NG, 2), np.arange(1, NG, 2)])
    eye = np.eye(TILE // NG, dtype=np.float32)
    sums = np.array([[1.0, 1.0], [1.0, -1.0]], np.float32)
    right_c = np.kron(np.eye(TILE // LANES, dtype=np.float32), np.kron(sums, table))
    left_b = np.kron(eye, table[order][:, order])
    halves = (table[0::2, :HALF], table[1::2, :HALF])
    rows = np.eye(TILE // HALF, dtype=np.float32)
    left_a = np.concatenate([np.kron(half, rows) for half in halves])
    back_a = np.concatenate([np.kron(half.T, rows) for half in halves])
    return jnp.asarray(np.concatenate([left_a, back_a, left_b, right_c])).astype(jnp.bfloat16)


def dot(left, right):
    return jnp.dot(left, right, preferred_element_type=jnp.float32)


def low(value):
    return value.astype(jnp.bfloat16)


def wide(value):
    return value.astype(jnp.float32)


def exchanged(first, second):
    lower = lax.broadcasted_iota(jnp.int32, first.shape, 1) < LANES // 2
    return (
        jnp.where(lower, first, pltpu.roll(second, LANES // 2, 1)),
        jnp.where(lower, pltpu.roll(first, LANES // 2, 1), second),
    )


def wavenum_sq(index):
    modes = wide(jnp.where(2 * index < NG, index, index - NG))
    wavenum = modes * (2.0 * math.pi / NG)
    return wavenum * wavenum


def screened_rows(group):
    shape = (TILE, LANES)
    row = lax.broadcasted_iota(jnp.int32, shape, 0)
    lane = lax.broadcasted_iota(jnp.int32, shape, 1)
    a = 2 * (row // SUB) + lane // NG
    place = group * SUB + row % SUB
    b = 2 * (place % HALF) + place // HALF
    norm_sq = wavenum_sq(a) + wavenum_sq(b) + wavenum_sq(lane % NG)
    bounded = jnp.where(norm_sq > 0, norm_sq, 1.0)
    screened = jnp.where(
        norm_sq > 0,
        4.0 * math.pi / bounded * (1.0 - jnp.exp(-bounded / (4.0 * OMEGA * OMEGA))),
        math.pi / (OMEGA * OMEGA),
    )
    return screened * (1.0 / NG**3)


def partner(me, step, count):
    total, bit = 0, 1
    while bit < count:
        total = total + bit * ((me // bit + step // bit) % 2)
        bit *= 2
    return total


def each(count, number, act):
    if count <= WRITTEN_OUT:
        for i in range(number):
            act(i)
    else:
        pl.loop(0, number)(act)


def grown(total, count):
    shift = LANES // 2
    while shift >= count:
        total = total + pltpu.roll(total, shift, 1)
        shift //= 2
    return total


def own_lanes(count):
    shape = (count, LANES)
    spread = LANES // count
    return (
        lax.broadcasted_iota(jnp.int32, shape, 0) % spread
        == lax.broadcasted_iota(jnp.int32, shape, 1) // count
    )


def own_columns(count):
    return lax.broadcasted_iota(jnp.int32, (count, TILE), 1) // count


def body(
    count,
    orb_hbm, tri_hbm, tables_hbm, occ,
    line_out, low_out, summed,
    factors,
    orb_line, tri_line, own, own_w, sibling, remote, tri_rows, kern, field, acc,
    e_rows, t_in, r_in, e_in, tt, et, exch_line, et_low, part, parts, total_here,
    load_sem, send_sem, recv_sem, orb_recv, e_recv, out_sem,
):
    me = lax.axis_index("band")
    flips = [bit * (1 - 2 * (me // bit % 2)) for bit in (1 << k for k in range(count.bit_length() - 1))]

    def mate(step):
        if isinstance(step, int):
            return me + sum(flip for k, flip in enumerate(flips) if step >> k & 1)
        return partner(me, step, count)

    barrier = pltpu.get_barrier_semaphore()
    slab = ROWS // count
    pack = TILE // count
    spread = LANES // count
    groups = slab // pack
    tiles = ROWS // TILE
    per_tile = TILE // NG
    depth = ROWS // CHUNKS
    span = HALF // CHUNKS * PLANE
    planes = max(count // 4, 1)
    sib = me + 1 - 2 * (me % 2)
    rem = (me + count - 1 + 2 * (me % 2)) % count
    left_a = factors.at[: 2 * TILE]
    back_a = factors.at[2 * TILE : 4 * TILE]
    left_b = factors.at[4 * TILE : 5 * TILE]
    right_c = factors.at[5 * TILE :]
    flat_t = tri_rows.reshape(ROWS, LANES)
    flat_e = e_rows.reshape(ROWS, LANES)

    far = planes - 1

    def far_steps(lows, act):
        def mixed(t):
            upper = t % far
            act((far - upper) * 4 + (t // far + upper) % lows)

        each(count, lows * far, mixed)

    def near_steps(act):
        for step in range(1, min(count, 4)):
            act(step)

    def load_orb(chunk, half):
        at = half * CHUNKS + chunk
        cut = pl.ds(at * span, span)
        return pltpu.make_async_copy(orb_hbm.at[:, cut], orb_line.at[:, cut], load_sem.at[at])

    def plane(ref, a):
        cut = pl.ds(pl.multiple_of(a * PLANE, PLANE), PLANE)
        return wide(ref[:, cut]).reshape(HALF, LANES)

    def remote_copy(src, dst, send, recv, peer):
        return pltpu.make_async_remote_copy(
            src_ref=src,
            dst_ref=dst,
            send_sem=send,
            recv_sem=recv,
            device_id={"band": peer},
            device_id_type=MESH,
        )

    def orbital(chunk):
        cut = pl.ds(chunk * depth, depth)
        return remote_copy(
            own_w.at[cut], remote.at[cut], send_sem.at[ORBITAL], orb_recv.at[chunk], rem
        )

    to_sibling = remote_copy(own_w, sibling, send_sem.at[SIBLING], recv_sem.at[SIBLING], sib)
    orbital_sent = remote_copy(own_w, remote, send_sem.at[ORBITAL], orb_recv.at[0], rem)

    def several(src, dst, kind, number):
        every = pl.ds(0, number)
        return remote_copy(src.at[every], dst.at[every], send_sem.at[kind], recv_sem.at[kind], sib)

    def trial_copy(step):
        peer = mate(step)
        return remote_copy(
            tri_rows.at[peer], t_in.at[me], send_sem.at[TRIAL], recv_sem.at[TRIAL], peer
        )

    def relayed(step):
        peer = mate(step)
        return remote_copy(
            tri_rows.at[mate(step + 2)], r_in.at[me], send_sem.at[RELAY], recv_sem.at[RELAY], peer
        )

    def onward(step):
        source = mate(step)
        return remote_copy(
            r_in.at[source], t_in.at[source], send_sem.at[ONWARD], recv_sem.at[TRIAL], mate(2)
        )

    def exchange_copy(peer, slot):
        return remote_copy(
            e_rows.at[peer], e_in.at[slot], send_sem.at[EXCHANGE], e_recv.at[slot], peer
        )

    def part_copy(peer):
        return remote_copy(part, parts.at[me], send_sem.at[PART], recv_sem.at[PART], peer)

    def tile(group):
        return pl.ds(pl.multiple_of(group * TILE, TILE), TILE)

    def two(read, step):
        return jnp.concatenate([read(2 * step), read(2 * step + 1)], axis=1)

    def halved(value):
        lane = lax.broadcasted_iota(jnp.int32, (TILE, TILE), 1)
        return jnp.where(lane % LANES < LANES // 2, value[:TILE], value[TILE:])

    def rise(weighted, start, stop):
        @pl.loop(start // 2, stop // 2, unroll=min(UNROLL, (stop - start) // 2))
        def _(step):
            density = two(
                lambda group: low(wide(own[tile(group), :]) * wide(weighted[tile(group), :])), step
            )
            value = dot(left_b[...], low(dot(density, right_c[...])))
            field[tile(2 * step), :] = value[:, :LANES]
            field[tile(2 * step + 1), :] = value[:, LANES:]

    def strip(a, group):
        return pl.ds(pl.multiple_of(a * NG + group * SUB, SUB), SUB)

    def turn(unroll):
        @pl.loop(0, tiles // 2, unroll=unroll)
        def _(step):
            value = two(
                lambda group: low(
                    jnp.concatenate([field[strip(a, group), :] for a in range(HALF)], axis=0)
                ),
                step,
            )
            value = low(halved(dot(left_a[...], value)))
            value = low(wide(value) * two(lambda group: kern[tile(group), :], step))
            value = low(halved(dot(back_a[...], value)))
            value = dot(value, right_c[...])
            for side in range(2):
                for a in range(HALF):
                    field[strip(a, 2 * step + side), :] = value[
                        a * SUB : (a + 1) * SUB, side * LANES : (side + 1) * LANES
                    ]

    def fall(weighted, step):
        value = dot(left_b[...], two(lambda group: low(field[tile(group), :]), step))
        return [
            value[:, side * LANES : (side + 1) * LANES] * wide(weighted[tile(2 * step + side), :])
            for side in range(2)
        ]

    load_tables = pltpu.make_async_copy(tables_hbm, factors, load_sem.at[2 * CHUNKS + 1])
    load_tri = pltpu.make_async_copy(tri_hbm, tri_line, load_sem.at[2 * CHUNKS])
    for chunk in range(CHUNKS):
        for half in range(2):
            load_orb(chunk, half).start()

    def greet(i):
        pl.semaphore_signal(
            barrier, inc=1, device_id={"band": mate(i + 1)}, device_id_type=MESH
        )

    each(count, count - 1, greet)

    fill = occ[0:1, :]
    for chunk in range(CHUNKS):
        for half in range(2):
            load_orb(chunk, half).wait()

        @pl.loop(chunk * HALF // CHUNKS, (chunk + 1) * HALF // CHUNKS, unroll=2)
        def _(a):
            pair = jnp.concatenate(exchanged(plane(orb_line, a), plane(orb_line, a + HALF)), axis=0)
            cut = pl.ds(pl.multiple_of(a * NG, NG), NG)
            own[cut, :] = low(pair)
            own_w[cut, :] = low(pair * fill)

    load_tri.start()
    load_tables.start()

    pl.semaphore_wait(barrier, count - 1)
    for chunk in range(CHUNKS):
        orbital(chunk).start()
    to_sibling.start()

    load_tri.wait()

    @pl.loop(0, NG, unroll=2)
    def _(a):
        flat_t[pl.ds(pl.multiple_of(a * HALF, HALF), HALF), :] = low(plane(tri_line, a))

    load_tables.wait()
    trial_copy(1).start()

    def send_trial(step):
        relayed(step).start()
        trial_copy(step).start()

    far_steps(2, send_trial)

    @pl.loop(0, tiles)
    def _(group):
        kern[tile(group), :] = screened_rows(group)

    rise(own_w, 0, tiles)
    turn(UNROLL)

    @pl.loop(0, tiles // 2, unroll=UNROLL)
    def _(step):
        for side, value in enumerate(fall(own_w, step)):
            acc[tile(2 * step + side), :] = value

    to_sibling.wait_recv()
    rise(sibling, 0, tiles)
    turn(UNROLL)

    @pl.loop(0, tiles // 2, unroll=UNROLL)
    def _(step):
        for side, value in enumerate(fall(sibling, step)):
            acc[tile(2 * step + side), :] += value

    for chunk in range(CHUNKS - 1):
        orbital(chunk).wait_recv()
        rise(remote, chunk * tiles // CHUNKS, (chunk + 1) * tiles // CHUNKS)
    orbital(CHUNKS - 1).wait_recv()
    for step in range(2, min(count, 4)):
        trial_copy(step).start()
    rise(remote, tiles - tiles // CHUNKS, tiles)
    turn(LAST_UNROLL)

    @pl.loop(0, tiles // 2, unroll=UNROLL)
    def _(step):
        for side, value in enumerate(fall(remote, step)):
            group = 2 * step + side
            value = -FRACTION * (acc[tile(group), :] + value)
            for j in range(per_tile):
                a = group * per_tile + j
                first, second = exchanged(
                    value[j * NG : j * NG + HALF], value[j * NG + HALF : (j + 1) * NG]
                )
                flat_e[pl.ds(pl.multiple_of(a * HALF, HALF), HALF), :] = low(first)
                flat_e[pl.ds(pl.multiple_of((a + HALF) * HALF, HALF), HALF), :] = low(second)

    t_in[pl.ds(me, 1)] = tri_rows[pl.ds(me, 1)]
    e_in[pl.ds(me, 1)] = e_rows[pl.ds(me, 1)]
    def send_exchange(step):
        exchange_copy(mate(step), me).start()

    near_steps(send_exchange)
    far_steps(4, send_exchange)

    def spread_out(src, dst, slot):
        dst[pl.ds(slot, slab, stride=count), :] = wide(src[slot])

    def take_exchange(step):
        peer = mate(step)
        exchange_copy(peer, peer).wait_recv()
        spread_out(e_in, et, peer)

    if far > 0:
        several(r_in, r_in, RELAY, 2 * far).wait_recv()
        far_steps(2, lambda step: onward(step).start())

    @pl.loop(0, NG, unroll=2)
    def _(a):
        cut = pl.ds(pl.multiple_of(a * PLANE, PLANE), PLANE)
        rows = wide(flat_e[pl.ds(pl.multiple_of(a * HALF, HALF), HALF), :])
        exch_line[:, cut] = low(rows.reshape(1, PLANE))

    store_line = pltpu.make_async_copy(exch_line, line_out, out_sem.at[0])
    store_low = pltpu.make_async_copy(et_low, low_out, out_sem.at[1])
    store_line.start()
    several(tri_rows, t_in, TRIAL, count - 1).wait_recv()

    @pl.loop(0, count)
    def _(slot):
        spread_out(t_in, tt, slot)

    spread_out(e_in, et, me)
    near_steps(take_exchange)
    far_steps(4, take_exchange)

    mine = [low(et[g * TILE : (g + 1) * TILE, :]) for g in range(groups)]
    for g in range(groups):
        et_low[g * TILE : (g + 1) * TILE, :] = mine[g]
    gram = lax.dot_general(
        jnp.concatenate([low(tt[g * TILE : (g + 1) * TILE, :]) for g in range(groups)], axis=1),
        jnp.concatenate(mine, axis=1),
        (((1,), (1,)), ((), ())),
        preferred_element_type=jnp.float32,
    )
    column = own_columns(count)
    total = jnp.zeros((count, TILE), jnp.float32)
    for r in range(pack):
        total = total + jnp.where(column == r, gram[r * count : (r + 1) * count], 0.0)
    total = grown(total[:, :LANES] + total[:, LANES:], count)
    if spread > 1:
        total = jnp.sum(
            jnp.where(own_lanes(count), total, 0.0).reshape(count // spread, spread, LANES), axis=1
        )
    part[...] = total
    parts[pl.ds(me, 1)] = total[None]

    each(count, count - 1, lambda i: part_copy(mate(count - 1 - i)).start())
    store_low.start()
    orbital_sent.wait_send()
    to_sibling.wait_send()
    several(tri_rows, t_in, TRIAL, count - 1 - 2 * far).wait_send()
    if far > 0:
        several(tri_rows, r_in, RELAY, 2 * far).wait_send()
        several(r_in, t_in, ONWARD, 2 * far).wait_send()
    several(e_rows, e_in, EXCHANGE, count - 1).wait_send()
    store_line.wait()
    store_low.wait()
    several(parts, parts, PART, count - 1).wait()
    total_here[...] = jnp.sum(parts[...], axis=0)
    store_sum = pltpu.make_async_copy(total_here, summed, out_sem.at[2])
    store_sum.start()
    store_sum.wait()


def finish(count, exch_line, et_low, summed, exch_hbm, proj_hbm, proj, out_sem):
    pack = TILE // count
    spread = LANES // count
    groups = ROWS // TILE
    width = pack * LANES
    store_exch = pltpu.make_async_copy(exch_line, exch_hbm, out_sem.at[groups])
    store_exch.start()
    total = summed[...] / math.sqrt(ROWS * LANES)
    if spread > 1:
        total = jnp.broadcast_to(total[:, None, :], (count // spread, spread, LANES))
        total = jnp.where(own_lanes(count), total.reshape(count, LANES), 0.0)
    total = grown(total, count)
    total = jnp.concatenate([total, total], axis=1)
    column = own_columns(count)
    mixing = low(
        jnp.concatenate([jnp.where(column == r, total, 0.0) for r in range(pack)], axis=0)
    )
    stores = []
    for group in range(groups):
        piece = dot(mixing, et_low[group * TILE : (group + 1) * TILE, :])
        piece = low(piece * (-1.0 / math.sqrt(count)))
        for r in range(pack):
            at = (group * pack + r) * LANES
            proj[:, at : at + LANES] = piece[r * count : (r + 1) * count]
        cut = pl.ds(group * width, width)
        stores.append(
            pltpu.make_async_copy(proj.at[:, cut], proj_hbm.at[:, cut], out_sem.at[group])
        )
        stores[-1].start()
    for store in stores:
        store.wait()
    store_exch.wait()


def local(orbitals, trial, occupations):
    count = lax.axis_size("band")
    cells = orbitals.shape[1]
    slab = ROWS // count
    rows = (ROWS, LANES)
    bf16, f32 = jnp.bfloat16, jnp.float32
    compact = (count // (LANES // count), LANES)
    dma = pltpu.SemaphoreType.DMA
    anywhere = pl.BlockSpec(memory_space=pl.ANY)
    vmem = pl.BlockSpec(memory_space=pltpu.VMEM)
    consts = tables()
    line, spread_low, summed = pl.pallas_call(
        functools.partial(body, count),
        out_shape=(
            jax.ShapeDtypeStruct((1, cells), bf16),
            jax.ShapeDtypeStruct(rows, bf16),
            jax.ShapeDtypeStruct(compact, f32),
        ),
        in_specs=[pl.BlockSpec(memory_space=pltpu.HBM)] * 3 + [vmem],
        out_specs=(anywhere, anywhere, anywhere),
        scratch_shapes=[
            pltpu.VMEM(consts.shape, bf16),
            pltpu.VMEM((1, cells), bf16),
            pltpu.VMEM((1, cells), bf16),
            pltpu.VMEM(rows, bf16),
            pltpu.VMEM(rows, bf16),
            pltpu.VMEM(rows, bf16),
            pltpu.VMEM(rows, bf16),
            pltpu.VMEM((count, slab, LANES), bf16),
            pltpu.VMEM(rows, f32),
            pltpu.VMEM(rows, f32),
            pltpu.VMEM(rows, f32),
            pltpu.VMEM((count, slab, LANES), bf16),
            pltpu.VMEM((count, slab, LANES), bf16),
            pltpu.VMEM((count, slab, LANES), bf16),
            pltpu.VMEM((count, slab, LANES), bf16),
            pltpu.VMEM(rows, f32),
            pltpu.VMEM(rows, f32),
            pltpu.VMEM((1, cells), bf16),
            pltpu.VMEM(rows, bf16),
            pltpu.VMEM(compact, f32),
            pltpu.VMEM((count,) + compact, f32),
            pltpu.VMEM(compact, f32),
            dma((2 * CHUNKS + 2,)),
            dma((KINDS,)),
            dma((KINDS,)),
            dma((CHUNKS,)),
            dma((count,)),
            dma((3,)),
        ],
        compiler_params=pltpu.CompilerParams(
            collective_id=1, has_side_effects=True, vmem_limit_bytes=VMEM_LIMIT
        ),
        name="exchange",
    )(
        *[pltpu.with_memory_space_constraint(x, pltpu.HBM) for x in (orbitals, trial, consts)],
        jnp.broadcast_to(occupations.astype(f32)[:, None], (8, LANES)),
    )
    return pl.pallas_call(
        functools.partial(finish, count),
        out_shape=(
            jax.ShapeDtypeStruct((1, cells), bf16),
            jax.ShapeDtypeStruct((count, cells // count), bf16),
        ),
        in_specs=[vmem, vmem, vmem],
        out_specs=(anywhere, anywhere),
        scratch_shapes=[
            pltpu.VMEM((count, cells // count), bf16),
            dma((ROWS // TILE + 1,)),
        ],
        compiler_params=pltpu.CompilerParams(vmem_limit_bytes=VMEM_LIMIT),
        name="finish",
    )(line, spread_low, summed)


def solution(mesh):
    return jax.shard_map(
        local,
        mesh=mesh,
        in_specs=(P(("spin", "band"), None), P(("spin", "band"), None), P(("spin", "band"))),
        out_specs=(P(("spin", "band"), None), P("spin", "band")),
        check_vma=False,
    )
```

time: 51.2 us -> 44 us (0.86)
  local copies, waits for them, and re-layouts: 3.79 us -> 0.01 us
  Pallas kernels: 46 us -> 42.5 us
    pallas_call x1, Pallas kernels: 46 us -> 41.2 us  [local(): pl.pallas_call(functools.partial(body, count), out_shape=(jax.ShapeDtypeS...]
    unnamed x4 -> x0, local copies, waits for them, and re-layouts: 3.79 us -> none
    pallas_call x0 -> x1, Pallas kernels: none -> 1.35 us  [local(): pl.pallas_call(functools.partial(finish, count), out_shape=(jax.ShapeDtyp...]
where the time goes in v3:
time: 44 us; the launch traced here: 43.8 us
  Pallas kernels  42.5 us (97%)
  between operations  1.29 us (3%)
    pallas_call x1, Pallas kernels, local(): pl.pallas_call(functools.partial(body, count), out_shape=(jax.ShapeDtypeS...  41.2 us
    pallas_call x1, Pallas kernels, local(): pl.pallas_call(functools.partial(finish, count), out_shape=(jax.ShapeDtyp...  1.35 us

profile of v3, /device:TPU:0, one launch (start us, length us, event | category | flops | bytes accessed | tf_op | source)
XLA Modules:
  0.0 43.8 jit_solution(254181827422558281)
XLA Ops:
  1.3 41.2 %exchange.1 = (bf16[1,262144]{1,0:T(2,128)(2,1)S(1)}, bf16[2048,128]{1,0:T(8,128)(2,1)S(1)}, f32[2,128]{1,0:T(2,128)S(1)}) custom-call(bf16[1,262144]{1,0:T(2,128)(2,1)} %orb_hbm.1, bf16[1,262144]{1,0:T(2,128)(2,1)} %tri_hbm.1, bf16[1536,256]{1,0:T(8,128)(2,1)} %constant.6.tables_hbm, f32[8,128]{1,0:T(8,128)S(1)} %broadcast_in_dim.9.occ), custom_call_target="tpu_custom_call" | custom-call | tf_op jit(solution)/shard_map/exchange/pallas_call | solution.py:502
  42.5 1.4 %finish.1 = (bf16[1,262144]{1,0:T(2,128)(2,1)}, bf16[16,16384]{1,0:T(8,128)(2,1)}) custom-call(bf16[1,262144]{1,0:T(2,128)(2,1)S(1)} %get-tuple-element.5.exch_line, bf16[2048,128]{1,0:T(8,128)(2,1)S(1)} %get-tuple-element.6.et_low, f32[2,128]{1,0:T(2,128)S(1)} %get-tuple-element.7.summed), custom_call_target="tpu_custom_call" | custom-call | tf_op jit(solution)/shard_map/finish/pallas_call | solution.py:549
  (1 shorter events, 0.0 us)

commit v4 on v3

--- a/solution.py
+++ b/solution.py
@@ -19,8 +19,9 @@
 LAST_UNROLL = 2
 VMEM_LIMIT = 30 << 20
 WRITTEN_OUT = 32
-ORBITAL, SIBLING, TRIAL, RELAY, ONWARD, EXCHANGE, PART = range(7)
-KINDS = 7
+PIECES = 1
+LOADS = 2
+OWN, TRIAL, PART, ONWARD, EXCHANGE = range(5)
 MESH = pl.DeviceIdType.MESH
 
 HALF = NG // 2
@@ -136,7 +137,7 @@
     factors,
     orb_line, tri_line, own, own_w, sibling, remote, tri_rows, kern, field, acc,
     e_rows, t_in, r_in, e_in, tt, et, exch_line, et_low, part, parts, total_here,
-    load_sem, send_sem, recv_sem, orb_recv, e_recv, out_sem,
+    load_sem, send_sem, recv_sem, orb_recv, r_recv, e_recv, out_sem,
 ):
     me = lax.axis_index("band")
     flips = [bit * (1 - 2 * (me // bit % 2)) for bit in (1 << k for k in range(count.bit_length() - 1))]
@@ -154,7 +155,7 @@
     tiles = ROWS // TILE
     per_tile = TILE // NG
     depth = ROWS // CHUNKS
-    span = HALF // CHUNKS * PLANE
+    span = HALF // LOADS * PLANE
     planes = max(count // 4, 1)
     sib = me + 1 - 2 * (me % 2)
     rem = (me + count - 1 + 2 * (me % 2)) % count
@@ -174,14 +175,20 @@
 
         each(count, lows * far, mixed)
 
+    def far_first(lows, act):
+        each(count, lows * far, lambda t: act((far - t // lows) * 4 + t % lows))
+
     def near_steps(act):
         for step in range(1, min(count, 4)):
             act(step)
 
-    def load_orb(chunk, half):
-        at = half * CHUNKS + chunk
-        cut = pl.ds(at * span, span)
-        return pltpu.make_async_copy(orb_hbm.at[:, cut], orb_line.at[:, cut], load_sem.at[at])
+    def load_orb(piece, half):
+        cut = pl.ds((half * LOADS + piece) * span, span)
+        return pltpu.make_async_copy(orb_hbm.at[:, cut], orb_line.at[:, cut], load_sem.at[piece])
+
+    def loaded_orb(piece):
+        cut = pl.ds(0, 2 * span)
+        return pltpu.make_async_copy(orb_hbm.at[:, cut], orb_line.at[:, cut], load_sem.at[piece])
 
     def plane(ref, a):
         cut = pl.ds(pl.multiple_of(a * PLANE, PLANE), PLANE)
@@ -200,15 +207,17 @@
     def orbital(chunk):
         cut = pl.ds(chunk * depth, depth)
         return remote_copy(
-            own_w.at[cut], remote.at[cut], send_sem.at[ORBITAL], orb_recv.at[chunk], rem
-        )
-
-    to_sibling = remote_copy(own_w, sibling, send_sem.at[SIBLING], recv_sem.at[SIBLING], sib)
-    orbital_sent = remote_copy(own_w, remote, send_sem.at[ORBITAL], orb_recv.at[0], rem)
+            own_w.at[cut], remote.at[cut], send_sem.at[OWN], orb_recv.at[chunk], rem
+        )
+
+    to_sibling = remote_copy(own_w, sibling, send_sem.at[OWN], recv_sem.at[OWN], sib)
+    own_sent = remote_copy(kern, field, send_sem.at[OWN], recv_sem.at[OWN], sib)
 
     def several(src, dst, kind, number):
         every = pl.ds(0, number)
-        return remote_copy(src.at[every], dst.at[every], send_sem.at[kind], recv_sem.at[kind], sib)
+        return remote_copy(
+            src.at[every], dst.at[every], send_sem.at[kind], recv_sem.at[min(kind, PART)], sib
+        )
 
     def trial_copy(step):
         peer = mate(step)
@@ -216,10 +225,13 @@
             tri_rows.at[peer], t_in.at[me], send_sem.at[TRIAL], recv_sem.at[TRIAL], peer
         )
 
-    def relayed(step):
-        peer = mate(step)
+    def relay_copy(step, slot):
         return remote_copy(
-            tri_rows.at[mate(step + 2)], r_in.at[me], send_sem.at[RELAY], recv_sem.at[RELAY], peer
+            tri_rows.at[mate(step + 2)],
+            r_in.at[slot],
+            send_sem.at[TRIAL],
+            r_recv.at[(step // 4 - 1) * 2 + step % 2],
+            mate(step),
         )
 
     def onward(step):
@@ -228,9 +240,10 @@
             r_in.at[source], t_in.at[source], send_sem.at[ONWARD], recv_sem.at[TRIAL], mate(2)
         )
 
-    def exchange_copy(peer, slot):
+    def exchange_copy(step, slot):
+        peer = mate(step)
         return remote_copy(
-            e_rows.at[peer], e_in.at[slot], send_sem.at[EXCHANGE], e_recv.at[slot], peer
+            e_rows.at[peer], e_in.at[slot], send_sem.at[EXCHANGE], e_recv.at[step - 1], peer
         )
 
     def part_copy(peer):
@@ -285,53 +298,53 @@
             for side in range(2)
         ]
 
-    load_tables = pltpu.make_async_copy(tables_hbm, factors, load_sem.at[2 * CHUNKS + 1])
-    load_tri = pltpu.make_async_copy(tri_hbm, tri_line, load_sem.at[2 * CHUNKS])
-    for chunk in range(CHUNKS):
-        for half in range(2):
-            load_orb(chunk, half).start()
+    load_tables = pltpu.make_async_copy(tables_hbm, factors, load_sem.at[LOADS + 1])
+    load_tri = pltpu.make_async_copy(tri_hbm, tri_line, load_sem.at[LOADS])
 
     def greet(i):
         pl.semaphore_signal(
             barrier, inc=1, device_id={"band": mate(i + 1)}, device_id_type=MESH
         )
 
-    each(count, count - 1, greet)
+    each(count, count - 1, lambda i: greet(count - 2 - i))
+
+    for piece in range(LOADS):
+        for half in range(2):
+            load_orb(piece, half).start()
+    load_tri.start()
+    load_tables.start()
 
     fill = occ[0:1, :]
-    for chunk in range(CHUNKS):
-        for half in range(2):
-            load_orb(chunk, half).wait()
-
-        @pl.loop(chunk * HALF // CHUNKS, (chunk + 1) * HALF // CHUNKS, unroll=2)
+    for piece in range(LOADS):
+        loaded_orb(piece).wait()
+
+        @pl.loop(piece * HALF // LOADS, (piece + 1) * HALF // LOADS, unroll=2)
         def _(a):
             pair = jnp.concatenate(exchanged(plane(orb_line, a), plane(orb_line, a + HALF)), axis=0)
             cut = pl.ds(pl.multiple_of(a * NG, NG), NG)
             own[cut, :] = low(pair)
             own_w[cut, :] = low(pair * fill)
 
-    load_tri.start()
-    load_tables.start()
-
+
+    load_tri.wait()
+
+    @pl.loop(0, NG, unroll=2)
+    def _(a):
+        flat_t[pl.ds(pl.multiple_of(a * HALF, HALF), HALF), :] = low(plane(tri_line, a))
+
+    load_tables.wait()
     pl.semaphore_wait(barrier, count - 1)
     for chunk in range(CHUNKS):
         orbital(chunk).start()
     to_sibling.start()
 
-    load_tri.wait()
-
-    @pl.loop(0, NG, unroll=2)
-    def _(a):
-        flat_t[pl.ds(pl.multiple_of(a * HALF, HALF), HALF), :] = low(plane(tri_line, a))
-
-    load_tables.wait()
     trial_copy(1).start()
 
     def send_trial(step):
-        relayed(step).start()
+        relay_copy(step, me).start()
         trial_copy(step).start()
 
-    far_steps(2, send_trial)
+    far_first(2, send_trial)
 
     @pl.loop(0, tiles)
     def _(group):
@@ -379,7 +392,7 @@
     t_in[pl.ds(me, 1)] = tri_rows[pl.ds(me, 1)]
     e_in[pl.ds(me, 1)] = e_rows[pl.ds(me, 1)]
     def send_exchange(step):
-        exchange_copy(mate(step), me).start()
+        exchange_copy(step, me).start()
 
     near_steps(send_exchange)
     far_steps(4, send_exchange)
@@ -389,12 +402,8 @@
 
     def take_exchange(step):
         peer = mate(step)
-        exchange_copy(peer, peer).wait_recv()
+        exchange_copy(step, peer).wait_recv()
         spread_out(e_in, et, peer)
-
-    if far > 0:
-        several(r_in, r_in, RELAY, 2 * far).wait_recv()
-        far_steps(2, lambda step: onward(step).start())
 
     @pl.loop(0, NG, unroll=2)
     def _(a):
@@ -405,11 +414,20 @@
     store_line = pltpu.make_async_copy(exch_line, line_out, out_sem.at[0])
     store_low = pltpu.make_async_copy(et_low, low_out, out_sem.at[1])
     store_line.start()
+    def pass_on(step):
+        relay_copy(step, mate(step)).wait_recv()
+        onward(step).start()
+
+    far_first(2, pass_on)
     several(tri_rows, t_in, TRIAL, count - 1).wait_recv()
 
-    @pl.loop(0, count)
+    @pl.loop(0, count, unroll=4)
     def _(slot):
-        spread_out(t_in, tt, slot)
+        spread_out(t_in, et, slot)
+
+    @pl.loop(0, tiles, unroll=4)
+    def _(group):
+        tt[tile(group), :] = low(et[tile(group), :])
 
     spread_out(e_in, et, me)
     near_steps(take_exchange)
@@ -419,7 +437,7 @@
     for g in range(groups):
         et_low[g * TILE : (g + 1) * TILE, :] = mine[g]
     gram = lax.dot_general(
-        jnp.concatenate([low(tt[g * TILE : (g + 1) * TILE, :]) for g in range(groups)], axis=1),
+        jnp.concatenate([tt[g * TILE : (g + 1) * TILE, :] for g in range(groups)], axis=1),
         jnp.concatenate(mine, axis=1),
         (((1,), (1,)), ((), ())),
         preferred_element_type=jnp.float32,
@@ -438,11 +456,9 @@
 
     each(count, count - 1, lambda i: part_copy(mate(count - 1 - i)).start())
     store_low.start()
-    orbital_sent.wait_send()
-    to_sibling.wait_send()
-    several(tri_rows, t_in, TRIAL, count - 1 - 2 * far).wait_send()
+    own_sent.wait_send()
+    several(tri_rows, t_in, TRIAL, count - 1).wait_send()
     if far > 0:
-        several(tri_rows, r_in, RELAY, 2 * far).wait_send()
         several(r_in, t_in, ONWARD, 2 * far).wait_send()
     several(e_rows, e_in, EXCHANGE, count - 1).wait_send()
     store_line.wait()
@@ -459,8 +475,16 @@
     spread = LANES // count
     groups = ROWS // TILE
     width = pack * LANES
-    store_exch = pltpu.make_async_copy(exch_line, exch_hbm, out_sem.at[groups])
-    store_exch.start()
+    stores = []
+    part = exch_line.shape[1] // PIECES
+    for piece in range(PIECES):
+        cut = pl.ds(piece * part, part)
+        stores.append(
+            pltpu.make_async_copy(
+                exch_line.at[:, cut], exch_hbm.at[:, cut], out_sem.at[groups + piece]
+            )
+        )
+        stores[-1].start()
     total = summed[...] / math.sqrt(ROWS * LANES)
     if spread > 1:
         total = jnp.broadcast_to(total[:, None, :], (count // spread, spread, LANES))
@@ -471,7 +495,6 @@
     mixing = low(
         jnp.concatenate([jnp.where(column == r, total, 0.0) for r in range(pack)], axis=0)
     )
-    stores = []
     for group in range(groups):
         piece = dot(mixing, et_low[group * TILE : (group + 1) * TILE, :])
         piece = low(piece * (-1.0 / math.sqrt(count)))
@@ -485,7 +508,6 @@
         stores[-1].start()
     for store in stores:
         store.wait()
-    store_exch.wait()
 
 
 def local(orbitals, trial, occupations):
@@ -524,18 +546,19 @@
             pltpu.VMEM((count, slab, LANES), bf16),
             pltpu.VMEM((count, slab, LANES), bf16),
             pltpu.VMEM((count, slab, LANES), bf16),
-            pltpu.VMEM(rows, f32),
+            pltpu.VMEM(rows, bf16),
             pltpu.VMEM(rows, f32),
             pltpu.VMEM((1, cells), bf16),
             pltpu.VMEM(rows, bf16),
             pltpu.VMEM(compact, f32),
             pltpu.VMEM((count,) + compact, f32),
             pltpu.VMEM(compact, f32),
-            dma((2 * CHUNKS + 2,)),
-            dma((KINDS,)),
-            dma((KINDS,)),
+            dma((LOADS + 2,)),
+            dma((5,)),
+            dma((3,)),
             dma((CHUNKS,)),
-            dma((count,)),
+            dma((max(2 * (count // 4 - 1), 1),)),
+            dma((count - 1,)),
             dma((3,)),
         ],
         compiler_params=pltpu.CompilerParams(
@@ -556,7 +579,7 @@
         out_specs=(anywhere, anywhere),
         scratch_shapes=[
             pltpu.VMEM((count, cells // count), bf16),
-            dma((ROWS // TILE + 1,)),
+            dma((ROWS // TILE + PIECES,)),
         ],
         compiler_params=pltpu.CompilerParams(vmem_limit_bytes=VMEM_LIMIT),
         name="finish",

time: 44 us -> 43.5 us (0.989)
  no operation moved by 1% of the time
where the time goes in v4:
time: 43.5 us; the launch traced here: 43.4 us
  Pallas kernels  42.1 us (97%)
  between operations  1.29 us (3%)
    pallas_call x1, Pallas kernels, local(): pl.pallas_call(functools.partial(body, count), out_shape=(jax.ShapeDtypeS...  40.7 us
    pallas_call x1, Pallas kernels, local(): pl.pallas_call(functools.partial(finish, count), out_shape=(jax.ShapeDtyp...  1.35 us

profile of v4, /device:TPU:0, one launch (start us, length us, event | category | flops | bytes accessed | tf_op | source)
XLA Modules:
  0.0 43.4 jit_solution(7271490899401720090)
XLA Ops:
  1.3 40.7 %exchange.1 = (bf16[1,262144]{1,0:T(2,128)(2,1)S(1)}, bf16[2048,128]{1,0:T(8,128)(2,1)S(1)}, f32[2,128]{1,0:T(2,128)S(1)}) custom-call(bf16[1,262144]{1,0:T(2,128)(2,1)} %orb_hbm.1, bf16[1,262144]{1,0:T(2,128)(2,1)} %tri_hbm.1, bf16[1536,256]{1,0:T(8,128)(2,1)} %constant.6.tables_hbm, f32[8,128]{1,0:T(8,128)S(1)} %broadcast_in_dim.9.occ), custom_call_target="tpu_custom_call" | custom-call | tf_op jit(solution)/shard_map/exchange/pallas_call | solution.py:524
  42.0 1.4 %finish.1 = (bf16[1,262144]{1,0:T(2,128)(2,1)}, bf16[16,16384]{1,0:T(8,128)(2,1)}) custom-call(bf16[1,262144]{1,0:T(2,128)(2,1)S(1)} %get-tuple-element.5.exch_line, bf16[2048,128]{1,0:T(8,128)(2,1)S(1)} %get-tuple-element.6.et_low, f32[2,128]{1,0:T(2,128)S(1)} %get-tuple-element.7.summed), custom_call_target="tpu_custom_call" | custom-call | tf_op jit(solution)/shard_map/finish/pallas_call | solution.py:572
  (1 shorter events, 0.0 us)

commit v5 on v4

--- a/solution.py
+++ b/solution.py
@@ -126,10 +126,6 @@
     )
 
 
-def own_columns(count):
-    return lax.broadcasted_iota(jnp.int32, (count, TILE), 1) // count
-
-
 def body(
     count,
     orb_hbm, tri_hbm, tables_hbm, occ,
@@ -149,9 +145,7 @@
 
     barrier = pltpu.get_barrier_semaphore()
     slab = ROWS // count
-    pack = TILE // count
     spread = LANES // count
-    groups = slab // pack
     tiles = ROWS // TILE
     per_tile = TILE // NG
     depth = ROWS // CHUNKS
@@ -171,7 +165,7 @@
     def far_steps(lows, act):
         def mixed(t):
             upper = t % far
-            act((far - upper) * 4 + (t // far + upper) % lows)
+            act((1 + upper) * 4 + (t // far + 2 * upper) % lows)
 
         each(count, lows * far, mixed)
 
@@ -433,20 +427,18 @@
     near_steps(take_exchange)
     far_steps(4, take_exchange)
 
-    mine = [low(et[g * TILE : (g + 1) * TILE, :]) for g in range(groups)]
-    for g in range(groups):
-        et_low[g * TILE : (g + 1) * TILE, :] = mine[g]
-    gram = lax.dot_general(
-        jnp.concatenate([tt[g * TILE : (g + 1) * TILE, :] for g in range(groups)], axis=1),
+    mine = [low(et[r * count : (r + 1) * count, :]) for r in range(slab)]
+    for r in range(slab):
+        et_low[r * count : (r + 1) * count, :] = mine[r]
+    total = lax.dot_general(
+        jnp.concatenate([tt[r * count : (r + 1) * count, :] for r in range(slab)], axis=1),
         jnp.concatenate(mine, axis=1),
         (((1,), (1,)), ((), ())),
         preferred_element_type=jnp.float32,
     )
-    column = own_columns(count)
-    total = jnp.zeros((count, TILE), jnp.float32)
-    for r in range(pack):
-        total = total + jnp.where(column == r, gram[r * count : (r + 1) * count], 0.0)
-    total = grown(total[:, :LANES] + total[:, LANES:], count)
+    if spread > 1:
+        rest = jnp.zeros((count, LANES - count), jnp.float32)
+        total = grown(jnp.concatenate([total, rest], axis=1), count)
     if spread > 1:
         total = jnp.sum(
             jnp.where(own_lanes(count), total, 0.0).reshape(count // spread, spread, LANES), axis=1
@@ -454,7 +446,12 @@
     part[...] = total
     parts[pl.ds(me, 1)] = total[None]
 
-    each(count, count - 1, lambda i: part_copy(mate(count - 1 - i)).start())
+    def send_part(peer):
+        @pl.when(peer != me)
+        def _():
+            part_copy(peer).start()
+
+    each(count, count, send_part)
     store_low.start()
     own_sent.wait_send()
     several(tri_rows, t_in, TRIAL, count - 1).wait_send()
@@ -490,17 +487,14 @@
         total = jnp.broadcast_to(total[:, None, :], (count // spread, spread, LANES))
         total = jnp.where(own_lanes(count), total.reshape(count, LANES), 0.0)
     total = grown(total, count)
-    total = jnp.concatenate([total, total], axis=1)
-    column = own_columns(count)
-    mixing = low(
-        jnp.concatenate([jnp.where(column == r, total, 0.0) for r in range(pack)], axis=0)
-    )
+    mixing = low(total[:, :count])
     for group in range(groups):
-        piece = dot(mixing, et_low[group * TILE : (group + 1) * TILE, :])
-        piece = low(piece * (-1.0 / math.sqrt(count)))
-        for r in range(pack):
+        for r in range(0, pack, 2):
+            row = (group * pack + r) * count
             at = (group * pack + r) * LANES
-            proj[:, at : at + LANES] = piece[r * count : (r + 1) * count]
+            sides = [et_low[row + k * count : row + (k + 1) * count, :] for k in range(2)]
+            piece = dot(mixing, jnp.concatenate(sides, axis=1))
+            proj[:, at : at + 2 * LANES] = low(piece * (-1.0 / math.sqrt(count)))
         cut = pl.ds(group * width, width)
         stores.append(
             pltpu.make_async_copy(proj.at[:, cut], proj_hbm.at[:, cut], out_sem.at[group])

time: 43.5 us -> 43 us (0.989)
  Pallas kernels: 42.1 us -> 41.6 us
where the time goes in v5:
time: 43 us; the launch traced here: 42.9 us
  Pallas kernels  41.6 us (97%)
  between operations  1.29 us (3%)
    pallas_call x1, Pallas kernels, local(): pl.pallas_call(functools.partial(body, count), out_shape=(jax.ShapeDtypeS...  40.4 us
    pallas_call x1, Pallas kernels, local(): pl.pallas_call(functools.partial(finish, count), out_shape=(jax.ShapeDtyp...  1.22 us

profile of v5, /device:TPU:0, one launch (start us, length us, event | category | flops | bytes accessed | tf_op | source)
XLA Modules:
  0.0 42.9 jit_solution(13737876313129383155)
XLA Ops:
  1.3 40.4 %exchange.1 = (bf16[1,262144]{1,0:T(2,128)(2,1)S(1)}, bf16[2048,128]{1,0:T(8,128)(2,1)S(1)}, f32[2,128]{1,0:T(2,128)S(1)}) custom-call(bf16[1,262144]{1,0:T(2,128)(2,1)} %orb_hbm.1, bf16[1,262144]{1,0:T(2,128)(2,1)} %tri_hbm.1, bf16[1536,256]{1,0:T(8,128)(2,1)} %constant.6.tables_hbm, f32[8,128]{1,0:T(8,128)S(1)} %broadcast_in_dim.9.occ), custom_call_target="tpu_custom_call" | custom-call | tf_op jit(solution)/shard_map/exchange/pallas_call | solution.py:518
  41.7 1.2 %finish.1 = (bf16[1,262144]{1,0:T(2,128)(2,1)}, bf16[16,16384]{1,0:T(8,128)(2,1)}) custom-call(bf16[1,262144]{1,0:T(2,128)(2,1)S(1)} %get-tuple-element.5.exch_line, bf16[2048,128]{1,0:T(8,128)(2,1)S(1)} %get-tuple-element.6.et_low, f32[2,128]{1,0:T(2,128)S(1)} %get-tuple-element.7.summed), custom_call_target="tpu_custom_call" | custom-call | tf_op jit(solution)/shard_map/finish/pallas_call | solution.py:566
  (1 shorter events, 0.0 us)

commit v6 on v5

--- a/solution.py
+++ b/solution.py
@@ -338,7 +338,9 @@
         relay_copy(step, me).start()
         trial_copy(step).start()
 
-    far_first(2, send_trial)
+    if far > 0:
+        for low_bit in range(2):
+            send_trial(far * 4 + low_bit)
 
     @pl.loop(0, tiles)
     def _(group):
@@ -352,6 +354,7 @@
         for side, value in enumerate(fall(own_w, step)):
             acc[tile(2 * step + side), :] = value
 
+    each(count, 2 * (far - 1), lambda t: send_trial((far - 1 - t // 2) * 4 + t % 2))
     to_sibling.wait_recv()
     rise(sibling, 0, tiles)
     turn(UNROLL)
@@ -412,7 +415,7 @@
         relay_copy(step, mate(step)).wait_recv()
         onward(step).start()
 
-    far_first(2, pass_on)
+    far_steps(2, pass_on)
     several(tri_rows, t_in, TRIAL, count - 1).wait_recv()
 
     @pl.loop(0, count, unroll=4)
@@ -438,11 +441,9 @@
     )
     if spread > 1:
         rest = jnp.zeros((count, LANES - count), jnp.float32)
-        total = grown(jnp.concatenate([total, rest], axis=1), count)
-    if spread > 1:
-        total = jnp.sum(
-            jnp.where(own_lanes(count), total, 0.0).reshape(count // spread, spread, LANES), axis=1
-        )
+        total = jnp.concatenate([total, rest], axis=1)
+        total = pltpu.roll(total, 0, 1, stride=count, stride_axis=0)
+        total = jnp.sum(total.reshape(count // spread, spread, LANES), axis=1)
     part[...] = total
     parts[pl.ds(me, 1)] = total[None]
 
@@ -478,7 +479,7 @@
         cut = pl.ds(piece * part, part)
         stores.append(
             pltpu.make_async_copy(
-                exch_line.at[:, cut], exch_hbm.at[:, cut], out_sem.at[groups + piece]
+                exch_line.at[:, cut], exch_hbm.at[:, cut], out_sem.at[groups // 2 + piece]
             )
         )
         stores[-1].start()
@@ -495,11 +496,12 @@
             sides = [et_low[row + k * count : row + (k + 1) * count, :] for k in range(2)]
             piece = dot(mixing, jnp.concatenate(sides, axis=1))
             proj[:, at : at + 2 * LANES] = low(piece * (-1.0 / math.sqrt(count)))
-        cut = pl.ds(group * width, width)
-        stores.append(
-            pltpu.make_async_copy(proj.at[:, cut], proj_hbm.at[:, cut], out_sem.at[group])
-        )
-        stores[-1].start()
+        if group % 2 == 1:
+            cut = pl.ds((group - 1) * width, 2 * width)
+            stores.append(
+                pltpu.make_async_copy(proj.at[:, cut], proj_hbm.at[:, cut], out_sem.at[group // 2])
+            )
+            stores[-1].start()
     for store in stores:
         store.wait()
 
@@ -573,7 +575,7 @@
         out_specs=(anywhere, anywhere),
         scratch_shapes=[
             pltpu.VMEM((count, cells // count), bf16),
-            dma((ROWS // TILE + PIECES,)),
+            dma((ROWS // TILE // 2 + PIECES,)),
         ],
         compiler_params=pltpu.CompilerParams(vmem_limit_bytes=VMEM_LIMIT),
         name="finish",

time: 43 us -> 42.9 us (level)
  no operation moved by 1% of the time
where the time goes in v6:
time: 42.9 us; the launch traced here: 42.7 us
  Pallas kernels  41.4 us (97%)
  between operations  1.29 us (3%)
    pallas_call x1, Pallas kernels, local(): pl.pallas_call(functools.partial(body, count), out_shape=(jax.ShapeDtypeS...  40.2 us
    pallas_call x1, Pallas kernels, local(): pl.pallas_call(functools.partial(finish, count), out_shape=(jax.ShapeDtyp...  1.2 us

profile of v6, /device:TPU:0, one launch (start us, length us, event | category | flops | bytes accessed | tf_op | source)
XLA Modules:
  0.0 42.7 jit_solution(4245141322736341123)
XLA Ops:
  1.3 40.2 %exchange.1 = (bf16[1,262144]{1,0:T(2,128)(2,1)S(1)}, bf16[2048,128]{1,0:T(8,128)(2,1)S(1)}, f32[2,128]{1,0:T(2,128)S(1)}) custom-call(bf16[1,262144]{1,0:T(2,128)(2,1)} %orb_hbm.1, bf16[1,262144]{1,0:T(2,128)(2,1)} %tri_hbm.1, bf16[1536,256]{1,0:T(8,128)(2,1)} %constant.6.tables_hbm, f32[8,128]{1,0:T(8,128)S(1)} %broadcast_in_dim.9.occ), custom_call_target="tpu_custom_call" | custom-call | tf_op jit(solution)/shard_map/exchange/pallas_call | solution.py:520
  41.5 1.2 %finish.1 = (bf16[1,262144]{1,0:T(2,128)(2,1)}, bf16[16,16384]{1,0:T(8,128)(2,1)}) custom-call(bf16[1,262144]{1,0:T(2,128)(2,1)S(1)} %get-tuple-element.5.exch_line, bf16[2048,128]{1,0:T(8,128)(2,1)S(1)} %get-tuple-element.6.et_low, f32[2,128]{1,0:T(2,128)S(1)} %get-tuple-element.7.summed), custom_call_target="tpu_custom_call" | custom-call | tf_op jit(solution)/shard_map/finish/pallas_call | solution.py:568
  (1 shorter events, 0.0 us)

commit v7 on v6

--- a/solution.py
+++ b/solution.py
@@ -224,7 +224,7 @@
             tri_rows.at[mate(step + 2)],
             r_in.at[slot],
             send_sem.at[TRIAL],
-            r_recv.at[(step // 4 - 1) * 2 + step % 2],
+            r_recv.at[step // 4 - 1],
             mate(step),
         )
 
@@ -295,6 +295,10 @@
     load_tables = pltpu.make_async_copy(tables_hbm, factors, load_sem.at[LOADS + 1])
     load_tri = pltpu.make_async_copy(tri_hbm, tri_line, load_sem.at[LOADS])
 
+    for piece in range(LOADS):
+        for half in range(2):
+            load_orb(piece, half).start()
+
     def greet(i):
         pl.semaphore_signal(
             barrier, inc=1, device_id={"band": mate(i + 1)}, device_id_type=MESH
@@ -302,9 +306,6 @@
 
     each(count, count - 1, lambda i: greet(count - 2 - i))
 
-    for piece in range(LOADS):
-        for half in range(2):
-            load_orb(piece, half).start()
     load_tri.start()
     load_tables.start()
 
@@ -338,9 +339,7 @@
         relay_copy(step, me).start()
         trial_copy(step).start()
 
-    if far > 0:
-        for low_bit in range(2):
-            send_trial(far * 4 + low_bit)
+    each(count, 2 * (far - 1), lambda t: send_trial((far - t // 2) * 4 + t % 2))
 
     @pl.loop(0, tiles)
     def _(group):
@@ -354,7 +353,9 @@
         for side, value in enumerate(fall(own_w, step)):
             acc[tile(2 * step + side), :] = value
 
-    each(count, 2 * (far - 1), lambda t: send_trial((far - 1 - t // 2) * 4 + t % 2))
+    if far > 0:
+        for low_bit in range(2):
+            send_trial(4 + low_bit)
     to_sibling.wait_recv()
     rise(sibling, 0, tiles)
     turn(UNROLL)
@@ -411,11 +412,15 @@
     store_line = pltpu.make_async_copy(exch_line, line_out, out_sem.at[0])
     store_low = pltpu.make_async_copy(et_low, low_out, out_sem.at[1])
     store_line.start()
-    def pass_on(step):
-        relay_copy(step, mate(step)).wait_recv()
-        onward(step).start()
-
-    far_steps(2, pass_on)
+    def pass_on(t):
+        two_slabs = pl.ds(0, 2)
+        remote_copy(
+            r_in.at[two_slabs], r_in.at[two_slabs], send_sem.at[TRIAL], r_recv.at[far - 1 - t], sib
+        ).wait_recv()
+        onward((far - t) * 4).start()
+        onward((far - t) * 4 + 1).start()
+
+    each(count, far, pass_on)
     several(tri_rows, t_in, TRIAL, count - 1).wait_recv()
 
     @pl.loop(0, count, unroll=4)
@@ -553,7 +558,7 @@
             dma((5,)),
             dma((3,)),
             dma((CHUNKS,)),
-            dma((max(2 * (count // 4 - 1), 1),)),
+            dma((max(count // 4 - 1, 1),)),
             dma((count - 1,)),
             dma((3,)),
         ],

time: 42.9 us -> 42.8 us (level)
  no operation moved by 1% of the time
where the time goes in v7:
time: 42.8 us; the launch traced here: 42.7 us
  Pallas kernels  41.4 us (97%)
  between operations  1.29 us (3%)
    pallas_call x1, Pallas kernels, local(): pl.pallas_call(functools.partial(body, count), out_shape=(jax.ShapeDtypeS...  40.2 us
    pallas_call x1, Pallas kernels, local(): pl.pallas_call(functools.partial(finish, count), out_shape=(jax.ShapeDtyp...  1.22 us

profile of v7, /device:TPU:0, one launch (start us, length us, event | category | flops | bytes accessed | tf_op | source)
XLA Modules:
  0.0 42.7 jit_solution(1554750751327205584)
XLA Ops:
  1.3 40.2 %exchange.1 = (bf16[1,262144]{1,0:T(2,128)(2,1)S(1)}, bf16[2048,128]{1,0:T(8,128)(2,1)S(1)}, f32[2,128]{1,0:T(2,128)S(1)}) custom-call(bf16[1,262144]{1,0:T(2,128)(2,1)} %orb_hbm.1, bf16[1,262144]{1,0:T(2,128)(2,1)} %tri_hbm.1, bf16[1536,256]{1,0:T(8,128)(2,1)} %constant.6.tables_hbm, f32[8,128]{1,0:T(8,128)S(1)} %broadcast_in_dim.9.occ), custom_call_target="tpu_custom_call" | custom-call | tf_op jit(solution)/shard_map/exchange/pallas_call | solution.py:525
  41.5 1.2 %finish.1 = (bf16[1,262144]{1,0:T(2,128)(2,1)}, bf16[16,16384]{1,0:T(8,128)(2,1)}) custom-call(bf16[1,262144]{1,0:T(2,128)(2,1)S(1)} %get-tuple-element.5.exch_line, bf16[2048,128]{1,0:T(8,128)(2,1)S(1)} %get-tuple-element.6.et_low, f32[2,128]{1,0:T(2,128)S(1)} %get-tuple-element.7.summed), custom_call_target="tpu_custom_call" | custom-call | tf_op jit(solution)/shard_map/finish/pallas_call | solution.py:573
  (1 shorter events, 0.0 us)

commit v8 on v6

--- a/solution.py
+++ b/solution.py
@@ -431,8 +431,6 @@
     far_steps(4, take_exchange)
 
     mine = [low(et[r * count : (r + 1) * count, :]) for r in range(slab)]
-    for r in range(slab):
-        et_low[r * count : (r + 1) * count, :] = mine[r]
     total = lax.dot_general(
         jnp.concatenate([tt[r * count : (r + 1) * count, :] for r in range(slab)], axis=1),
         jnp.concatenate(mine, axis=1),
@@ -453,6 +451,11 @@
             part_copy(peer).start()
 
     each(count, count, send_part)
+
+    @pl.loop(0, tiles, unroll=4)
+    def _(group):
+        et_low[tile(group), :] = low(et[tile(group), :])
+
     store_low.start()
     own_sent.wait_send()
     several(tri_rows, t_in, TRIAL, count - 1).wait_send()

time: 42.9 us -> 42.9 us (level)
  no operation moved by 1% of the time
where the time goes in v8:
time: 42.9 us; the launch traced here: 42.7 us
  Pallas kernels  41.4 us (97%)
  between operations  1.29 us (3%)
    pallas_call x1, Pallas kernels, local(): pl.pallas_call(functools.partial(body, count), out_shape=(jax.ShapeDtypeS...  40.2 us
    pallas_call x1, Pallas kernels, local(): pl.pallas_call(functools.partial(finish, count), out_shape=(jax.ShapeDtyp...  1.21 us

profile of v8, /device:TPU:0, one launch (start us, length us, event | category | flops | bytes accessed | tf_op | source)
XLA Modules:
  0.0 42.7 jit_solution(10938602284746784454)
XLA Ops:
  1.3 40.2 %exchange.1 = (bf16[1,262144]{1,0:T(2,128)(2,1)S(1)}, bf16[2048,128]{1,0:T(8,128)(2,1)S(1)}, f32[2,128]{1,0:T(2,128)S(1)}) custom-call(bf16[1,262144]{1,0:T(2,128)(2,1)} %orb_hbm.1, bf16[1,262144]{1,0:T(2,128)(2,1)} %tri_hbm.1, bf16[1536,256]{1,0:T(8,128)(2,1)} %constant.6.tables_hbm, f32[8,128]{1,0:T(8,128)S(1)} %broadcast_in_dim.9.occ), custom_call_target="tpu_custom_call" | custom-call | tf_op jit(solution)/shard_map/exchange/pallas_call | solution.py:523
  41.5 1.2 %finish.1 = (bf16[1,262144]{1,0:T(2,128)(2,1)}, bf16[16,16384]{1,0:T(8,128)(2,1)}) custom-call(bf16[1,262144]{1,0:T(2,128)(2,1)S(1)} %get-tuple-element.5.exch_line, bf16[2048,128]{1,0:T(8,128)(2,1)S(1)} %get-tuple-element.6.et_low, f32[2,128]{1,0:T(2,128)S(1)} %get-tuple-element.7.summed), custom_call_target="tpu_custom_call" | custom-call | tf_op jit(solution)/shard_map/finish/pallas_call | solution.py:571
  (1 shorter events, 0.0 us)

commit v9 on v8

--- a/solution.py
+++ b/solution.py
@@ -338,9 +338,7 @@
         relay_copy(step, me).start()
         trial_copy(step).start()
 
-    if far > 0:
-        for low_bit in range(2):
-            send_trial(far * 4 + low_bit)
+    each(count, 2 * (far - 1), lambda t: send_trial((far - t // 2) * 4 + t % 2))
 
     @pl.loop(0, tiles)
     def _(group):
@@ -354,7 +352,9 @@
         for side, value in enumerate(fall(own_w, step)):
             acc[tile(2 * step + side), :] = value
 
-    each(count, 2 * (far - 1), lambda t: send_trial((far - 1 - t // 2) * 4 + t % 2))
+    if far > 0:
+        for low_bit in range(2):
+            send_trial(4 + low_bit)
     to_sibling.wait_recv()
     rise(sibling, 0, tiles)
     turn(UNROLL)

time: 42.9 us -> 42.9 us (level)
  no operation moved by 1% of the time
where the time goes in v9:
time: 42.9 us; the launch traced here: 42.7 us
  Pallas kernels  41.4 us (97%)
  between operations  1.29 us (3%)
    pallas_call x1, Pallas kernels, local(): pl.pallas_call(functools.partial(body, count), out_shape=(jax.ShapeDtypeS...  40.2 us
    pallas_call x1, Pallas kernels, local(): pl.pallas_call(functools.partial(finish, count), out_shape=(jax.ShapeDtyp...  1.22 us

profile of v9, /device:TPU:0, one launch (start us, length us, event | category | flops | bytes accessed | tf_op | source)
XLA Modules:
  0.0 42.7 jit_solution(8824688180489316043)
XLA Ops:
  1.3 40.2 %exchange.1 = (bf16[1,262144]{1,0:T(2,128)(2,1)S(1)}, bf16[2048,128]{1,0:T(8,128)(2,1)S(1)}, f32[2,128]{1,0:T(2,128)S(1)}) custom-call(bf16[1,262144]{1,0:T(2,128)(2,1)} %orb_hbm.1, bf16[1,262144]{1,0:T(2,128)(2,1)} %tri_hbm.1, bf16[1536,256]{1,0:T(8,128)(2,1)} %constant.6.tables_hbm, f32[8,128]{1,0:T(8,128)S(1)} %broadcast_in_dim.9.occ), custom_call_target="tpu_custom_call" | custom-call | tf_op jit(solution)/shard_map/exchange/pallas_call | solution.py:523
  41.5 1.2 %finish.1 = (bf16[1,262144]{1,0:T(2,128)(2,1)}, bf16[16,16384]{1,0:T(8,128)(2,1)}) custom-call(bf16[1,262144]{1,0:T(2,128)(2,1)S(1)} %get-tuple-element.5.exch_line, bf16[2048,128]{1,0:T(8,128)(2,1)S(1)} %get-tuple-element.6.et_low, f32[2,128]{1,0:T(2,128)S(1)} %get-tuple-element.7.summed), custom_call_target="tpu_custom_call" | custom-call | tf_op jit(solution)/shard_map/finish/pallas_call | solution.py:571
  (1 shorter events, 0.0 us)
